TPU v7x, 128 devices: a 2x2x16 block of a 8x8x16 slice. The times are simulated.
128 devices in a mesh: groups: 4 (over x, y), blk: 32 (over z, core).
Axes of the slice: x: 2, y: 2, z: 16, core: 2. Of those that a mesh axis runs over, the one named last changes fastest.
The devices are a block of a 8x8x16 slice.
Arguments:
- coords: float32 [32, 98304], P(None, ('groups', 'blk')), parts along dimension 1, may hold values from -6 to 6
- alpha: float32 [98304], P(('groups', 'blk')), parts along dimension 0, may hold values from -6 to 6
- probe_solves: float32 [15, 98304], P(None, ('groups', 'blk')), parts along dimension 1, may hold values from -6 to 6
- probes: float32 [15, 98304], P(None, ('groups', 'blk')), parts along dimension 1, may hold values from -6 to 6
- lengthscale: float32 [32], replicated, may hold values from 4 to 12
Outputs:
- grad: float32 [32, 98304], P(None, ('groups', 'blk')), parts along dimension 1
There are 4 independent parts, one for each index of `groups`. A program takes and returns all parts, laid end to end along the dimension named above; an argument that names none is the same for every part. Nothing has to cross between parts.
All inputs are finite; a program needn't handle non-finite values.
Results may differ from a plain program's by a relative error of at most 0.00014.
Values sent between devices are 32-bit elements; how exact they have to be, the bound alone decides.
No kernel may reach another device: no remote copies, remote signals or barrier semaphores. Data moves between devices by JAX's collectives and lax.ppermute only.
A program may use at most 64 MiB of HBM per device.

v0:
```python
import functools

import jax
import jax.numpy as jnp
from jax import lax
from jax.experimental import pallas as pl
from jax.experimental.pallas import tpu as pltpu
from jax.sharding import PartitionSpec as P

root_five = 5.0**0.5
minus_log2e = -1.4426950408889634
f32, bf16 = jnp.float32, jnp.bfloat16
VMEM = pl.BlockSpec(memory_space=pltpu.VMEM)
DIM, GROUP, SUMS = 32, 16, 80
STEP, BACK, AHEAD, LAG = 128, 256, 1, 2


def halves(value):
    high = value.astype(bf16)
    return high, (value - high.astype(f32)).astype(bf16)


def row_is(row, value, other):
    return jnp.where(lax.broadcasted_iota(jnp.int32, other.shape, 0) == row, value, other)


def edge_rows(square, parts_at, ones_at):
    one = square.astype(bf16).astype(f32)
    rest = square - one
    two = rest.astype(bf16).astype(f32)
    row = lax.broadcasted_iota(jnp.int32, square.shape, 0)
    edge = jnp.where((row >= ones_at) & (row < ones_at + 3), 1.0, 0.0)
    for index, part in enumerate((one, two, rest - two)):
        edge = row_is(parts_at + index, part, edge)
    return edge.astype(bf16)


def own_forms(field, dist_ref, coup_ref):
    high, low = halves(field[:DIM])
    first, second = field[DIM : DIM + GROUP], field[DIM + GROUP :]
    square = jnp.broadcast_to(second[:1], first.shape)
    dist_ref[...] = jnp.concatenate([high, low, high, low, edge_rows(square, 3, 0)], 0)
    table = jnp.concatenate([row_is(0, first, second), row_is(0, 0.0, first)], 0)
    high, low = halves(table)
    coup_ref[...] = jnp.concatenate([high, low, high, low], 0)


def visit_forms(half_inv, field, dist_ref, coup_ref, sums_ref):
    points = field.shape[1]
    high, low = halves(field[:DIM])
    first, second = field[DIM : DIM + GROUP], field[DIM + GROUP :]
    sums_ref[...] = jnp.concatenate([high, low, jnp.ones((GROUP, points), bf16)], 0)
    square = jnp.broadcast_to(second[:1], first.shape)
    twice = [-2.0 * high, -2.0 * low]
    zero = jnp.zeros((256 - 4 * DIM - GROUP, points), bf16)
    dist = jnp.concatenate([*twice, *twice[::-1], edge_rows(square, 0, 3), zero], 0)
    dist_ref[...] = dist.T
    table = jnp.concatenate(
        [row_is(0, first, -half_inv * first), row_is(0, 0.0, -half_inv * second)], 0
    )
    high, low = halves(table)
    coup_ref[...] = jnp.concatenate([high, high, low, low], 0).T


def weights(dist, coup):
    dist = jnp.maximum(dist, 1e-30)
    scaled = dist * lax.rsqrt(dist)
    return coup * ((1.0 + scaled) * jnp.exp2(scaled * minus_log2e))


def dot(left, right):
    return lax.dot_general(
        left, right, (((1,), (0,)), ((), ())), preferred_element_type=f32
    )


def add_tiles(pairs, sides, own, accs, high_ref, low_ref):
    points = accs[0].shape[1]
    width = high_ref.shape[2]
    depth = own[0][0].shape[0]
    chunks = [
        (v, o, start, begin)
        for v, o in pairs
        for start in range(0, points, width)
        for begin in range(0, points, STEP)
    ]

    def front(chunk):
        v, o, start, begin = chunk
        rows, cols = slice(begin, begin + STEP), slice(start, start + width)
        return (
            dot(sides[v][0][rows, :depth], own[o][0][:, cols]),
            dot(sides[v][1][rows, :], own[o][1][:, cols]),
        )

    def middle(chunk, products, slot):
        v, o, start, begin = chunk
        rows = slice(begin, begin + STEP)
        high, low = halves(weights(*products))
        high_ref[slot, rows, :] = high
        low_ref[slot, rows, :] = low

    def back(chunk, slot):
        v, o, start, begin = chunk
        sums = sides[v][2][:, begin : begin + BACK]
        rows, cols = slice(begin, begin + BACK), slice(start, start + width)
        accs[o][:, cols] += dot(sums, high_ref[slot, rows, :]) + dot(sums, low_ref[slot, rows, :])

    per = points // STEP
    slot_of = lambda index: (index // per) % 2
    per_back = BACK // STEP
    products = {}
    for index in range(min(AHEAD, len(chunks))):
        products[index] = front(chunks[index])
    for index, chunk in enumerate(chunks):
        if index + AHEAD < len(chunks):
            products[index + AHEAD] = front(chunks[index + AHEAD])
        middle(chunk, products.pop(index), slot_of(index))
        late = index - LAG
        if late >= 0 and late % per_back == per_back - 1:
            first = late - per_back + 1
            back(chunks[first], slot_of(first))
    for late in range(len(chunks) - LAG, len(chunks)):
        if late % per_back == per_back - 1:
            first = late - per_back + 1
            back(chunks[first], slot_of(first))


def finish(field, acc):
    high, low = halves(field[:DIM])
    near = high.astype(f32) + low.astype(f32)
    return near * acc[2 * DIM : 2 * DIM + 1] - (acc[:DIM] + acc[DIM : 2 * DIM])


def visit_kernel(half_inv, pairs, n_vis, n_own, n_acc, n_form, done, *refs):
    refs = list(refs)

    def take(count):
        taken, refs[:] = refs[:count], refs[count:]
        return taken

    vis = take(n_vis)
    own = [take(2) for _ in range(n_own)]
    acc_in = take(n_acc)
    fields = take(len(done))
    acc_out = take(n_own)
    forms = [take(2) for _ in range(n_form)]
    outs = take(len(done))
    high_ref, low_ref = take(2)
    for index in range(n_own):
        if index < n_acc:
            acc_out[index][...] = acc_in[index][...]
        else:
            acc_out[index][...] = jnp.zeros_like(acc_out[index])
    for index in range(n_form):
        own_forms(vis[index][...], *forms[index])
    sides = []
    for ref in vis:
        side = take(3)
        visit_forms(half_inv, ref[...], *side)
        sides.append(side)
    add_tiles(pairs, sides, own, acc_out, high_ref, low_ref)
    for o, field, out in zip(done, fields, outs):
        out[...] = finish(field[...], acc_out[o][...])


def visit(half_inv, pairs, vis, own, accs, n_form=0, done=(), fields=()):
    points = vis[0].shape[1]
    n_own = len(own)
    acc_shape = jax.ShapeDtypeStruct((SUMS, points), f32)
    form_shapes = [
        jax.ShapeDtypeStruct((4 * DIM + GROUP, points), bf16),
        jax.ShapeDtypeStruct((8 * GROUP, points), bf16),
    ]
    out_shape = [acc_shape] * n_own + form_shapes * n_form
    out_shape += [jax.ShapeDtypeStruct((DIM, points), f32)] * len(done)
    scratch = [pltpu.VMEM((2, points, 256), bf16)] * 2
    for _ in vis:
        scratch += [
            pltpu.VMEM((points, 256), bf16),
            pltpu.VMEM((points, 8 * GROUP), bf16),
            pltpu.VMEM((SUMS, points), bf16),
        ]
    args = [*vis, *[ref for forms in own for ref in forms], *accs, *fields]
    first = len(vis) + 2 * n_own
    return pl.pallas_call(
        functools.partial(
            visit_kernel, half_inv, pairs, len(vis), n_own, len(accs), n_form, done
        ),
        out_shape=out_shape,
        in_specs=[VMEM] * len(args),
        out_specs=[VMEM] * len(out_shape),
        scratch_shapes=scratch,
        input_output_aliases={first + index: index for index in range(len(accs))},
        compiler_params=pltpu.CompilerParams(vmem_limit_bytes=20 * 2**20),
        cost_estimate=pl.CostEstimate(
            flops=len(pairs) * 10**9, bytes_accessed=10**6, transcendentals=0
        ),
        name="visit",
    )(*args)


def field_kernel(coords, alpha, solves, probes, length, field, dist_ref, coup_ref):
    size = length.shape[1]
    spread = jnp.broadcast_to(length[...], (size, size))
    row = lax.broadcasted_iota(jnp.int32, (size, size), 0)
    col = lax.broadcasted_iota(jnp.int32, (size, size), 1)
    column = jnp.sum(jnp.where(row == col, spread, 0.0), 1, keepdims=True)
    scaled = coords[...] * (1.0 / column)
    high, low = halves(scaled)
    near = high.astype(f32) + low.astype(f32)
    middle = DIM + GROUP
    lanes = alpha.shape[1]
    field[0:DIM, :] = scaled
    for index in range(alpha.shape[0]):
        field[DIM : DIM + 1, index * lanes : (index + 1) * lanes] = alpha[index : index + 1, :]
    field[DIM + 1 : middle, :] = solves[...]
    field[middle : middle + 1, :] = jnp.sum(near * near, 0, keepdims=True)
    field[middle + 1 :, :] = probes[...]
    own_forms(field[...], dist_ref, coup_ref)


def make_field(coords, alpha, solves, probes, lengthscale):
    points = coords.shape[1]
    args = (coords * root_five, alpha.reshape(-1, 128), solves, probes, lengthscale[None])
    return pl.pallas_call(
        field_kernel,
        out_shape=[
            jax.ShapeDtypeStruct((DIM + 2 * GROUP, points), f32),
            jax.ShapeDtypeStruct((4 * DIM + GROUP, points), bf16),
            jax.ShapeDtypeStruct((8 * GROUP, points), bf16),
        ],
        in_specs=[VMEM] * 5,
        out_specs=[VMEM] * 3,
        compiler_params=pltpu.CompilerParams(vmem_limit_bytes=8 * 2**20),
        name="field",
    )(*args)


def swapped(value):
    count = lax.axis_size("blk")
    return lax.ppermute(value, "blk", [(b, b + 1 - 2 * (b % 2)) for b in range(count)])


def toward(value, even, odd):
    count = lax.axis_size("blk")
    pairs = [(b, (b + (odd if b % 2 else even)) % count) for b in range(count)]
    return lax.ppermute(value, "blk", pairs)


def on_device(coords, alpha, probe_solves, probes, lengthscale):
    half_inv = 1.0 / (2.0 * probes.shape[0])
    hops = lax.axis_size("blk") // 8
    field, *own = make_field(coords, alpha, probe_solves, probes, lengthscale)
    mate = swapped(field)
    near = toward(field, -2, 2)
    acc, *own_mate = visit(half_inv, ((0, 0),), [mate], [own], [], n_form=1)
    later, acc = lax.optimization_barrier((field, acc))
    cross = toward(later, 3, -3)
    near, acc = lax.optimization_barrier((near, acc))
    accs = [acc]
    for hop in range(1, hops):
        here, there = near, cross
        near = toward(here, -2, 2)
        accs = visit(half_inv, ((0, 1), (0, 0)), [here], [own, own_mate], accs)
        there, near_accs = lax.optimization_barrier((there, accs))
        cross = toward(there, -2, 2)
        accs = visit(half_inv, ((0, 1), (0, 0)), [there], [own, own_mate], near_accs)
    (acc,) = visit(half_inv, ((0, 0),), [near], [own_mate], accs[1:])
    cross, acc = lax.optimization_barrier((cross, acc))
    _, theirs = visit(half_inv, ((0, 0),), [cross], [own_mate], [acc], done=(0,), fields=[mate])
    theirs = swapped(theirs)
    _, mine = visit(half_inv, ((0, 0),), [near], [own], accs[:1], done=(0,), fields=[field])
    total = mine + theirs
    return (-(root_five / 3.0) / lengthscale)[:, None] * total


def solution(mesh):
    return jax.shard_map(
        on_device,
        mesh=mesh,
        in_specs=(
            P(None, ("groups", "blk")),
            P(("groups", "blk")),
            P(None, ("groups", "blk")),
            P(None, ("groups", "blk")),
            P(),
        ),
        out_specs=P(None, ("groups", "blk")),
        check_vma=False,
    )
```

profile of v0, /device:TPU:69, one launch (start us, length us, event | category | flops | bytes accessed | tf_op | source)
XLA Modules:
  0.0 51.2 jit_solution(14145891158696512133)
XLA Ops:
  0.0 0.9 %broadcast_multiply_fusion.coords = f32[32,768]{1,0:T(8,128)S(1)} fusion(f32[32,768]{1,0:T(8,128)} %param.5), kind=kLoop, calls=%fused_computation.1 | loop fusion | flops 24576 | bytes 196608 | tf_op jit(solution)/shard_map/mul | solution.py:225
  1.0 0.6 %copy-done.3 = f32[32]{0:T(128)S(1)} copy-done((f32[32]{0:T(128)S(1)}, f32[32]{0:T(128)}, u32[]{:S(2)}) %copy-start.3) | copy-done | bytes 152
  1.7 10.0 %collective-permute-start.1 = (f32[64,768]{1,0:T(8,128)S(1)}, f32[64,768]{1,0:T(8,128)S(1)}, u32[]{:S(2)}, u32[]{:S(2)}) collective-permute-start(f32[64,768]{1,0:T(8,128)S(1)} %get-tuple-element.46.refs_4_), channel_id=1, source_target_pairs={{0,1},{1,0},{2,3},{3,2},{4,5},{5,4},{6,7},{7,6},{8,9},{9,8},{10,11... | collective-permute-start | bytes 589832 | tf_op jit(solution)/shard_map/ppermute | solution.py:242
  11.8 1.1 %collective-permute-done.1.refs_0_.refs_4_ = f32[64,768]{1,0:T(8,128)S(1)} collective-permute-done((f32[64,768]{1,0:T(8,128)S(1)}, f32[64,768]{1,0:T(8,128)S(1)}, u32[]{:S(2)}, u32[]{:S(2)}) %collective-permute-start.1) | collective-permute-done | bytes 196640 | tf_op jit(solution)/shard_map/ppermute | solution.py:242
  12.8 1.5 %visit.10 = (f32[80,768]{1,0:T(8,128)S(1)}, bf16[144,768]{1,0:T(8,128)(2,1)S(1)}, bf16[128,768]{1,0:T(8,128)(2,1)S(1)}) custom-call(f32[64,768]{1,0:T(8,128)S(1)} %collective-permute-done.1.refs_0_.refs_4_, bf16[144,768]{1,0:T(8,128)(2,1)S(1)} %get-tuple-element.41.refs_1_, bf16[128,768]{1,0:T(8,128)(2,1)S(1)} %get-tuple-element.42.refs_2_), custom_call_target="tpu_custom_call" | custom-call | flops 1000000000 | bytes 1000000 | tf_op jit(solution)/shard_map/visit/pallas_call | solution.py:186
  14.4 4.2 %collective-permute-start.5 = (f32[64,768]{1,0:T(8,128)S(1)}, f32[64,768]{1,0:T(8,128)S(1)}, u32[]{:S(2)}, u32[]{:S(2)}) collective-permute-start(f32[64,768]{1,0:T(8,128)S(1)} %get-tuple-element.46.refs_4_), channel_id=1, source_target_pairs={{0,3},{1,30},{2,5},{3,0},{4,7},{5,2},{6,9},{7,4},{8,11},{9,6},{10,... | collective-permute-start | bytes 589832 | tf_op jit(solution)/shard_map/ppermute | solution.py:248
  18.6 0.4 collective-permute-start.2
  19.0 2.7 %visit.11 = (f32[80,768]{1,0:T(8,128)S(1)}, f32[80,768]{1,0:T(8,128)S(1)}) custom-call(f32[64,768]{1,0:T(8,128)S(1)} %collective-permute-done.refs_0_, bf16[144,768]{1,0:T(8,128)(2,1)S(1)} %get-tuple-element.41.refs_1_, bf16[128,768]{1,0:T(8,128)(2,1)S(1)} %get-tuple-element.42.refs_2_, ...), custom_call_target="tpu_custom_call", output_to_operand_aliasing={{0}: (5, {})} | custom-call | flops 2000000000 | bytes 1000000 | tf_op jit(solution)/shard_map/visit/pallas_call | solution.py:186
  21.6 0.3 collective-permute-done.5.refs_0_
  21.9 1.4 %collective-permute-start.6 = (f32[64,768]{1,0:T(8,128)S(1)}, f32[64,768]{1,0:T(8,128)S(1)}, u32[]{:S(2)}, u32[]{:S(2)}) collective-permute-start(f32[64,768]{1,0:T(8,128)S(1)} %collective-permute-done.5.refs_0_), channel_id=1, source_target_pairs={{0,30},{1,3},{2,0},{3,5},{4,2},{5,7},{6,4},{7,9},{8,6},{9,11},{10,... | collective-permute-start | bytes 589832 | tf_op jit(solution)/shard_map/ppermute | solution.py:248
  23.3 2.7 %visit.12 = (f32[80,768]{1,0:T(8,128)S(1)}, f32[80,768]{1,0:T(8,128)S(1)}) custom-call(f32[64,768]{1,0:T(8,128)S(1)} %collective-permute-done.5.refs_0_, bf16[144,768]{1,0:T(8,128)(2,1)S(1)} %get-tuple-element.41.refs_1_, bf16[128,768]{1,0:T(8,128)(2,1)S(1)} %get-tuple-element.42.refs_2_, ...), custom_call_target="tpu_custom_call", output_to_operand_aliasing={{0}: (5, {}), {1}: (6, {})} | custom-call | flops 2000000000 | bytes 1000000 | tf_op jit(solution)/shard_map/visit/pallas_call | solution.py:186
  26.1 2.7 %visit.13 = (f32[80,768]{1,0:T(8,128)S(1)}, f32[80,768]{1,0:T(8,128)S(1)}) custom-call(f32[64,768]{1,0:T(8,128)S(1)} %collective-permute-done.2.refs_0_, bf16[144,768]{1,0:T(8,128)(2,1)S(1)} %get-tuple-element.41.refs_1_, bf16[128,768]{1,0:T(8,128)(2,1)S(1)} %get-tuple-element.42.refs_2_, ...), custom_call_target="tpu_custom_call", output_to_operand_aliasing={{0}: (5, {}), {1}: (6, {})} | custom-call | flops 2000000000 | bytes 1000000 | tf_op jit(solution)/shard_map/visit/pallas_call | solution.py:186
  28.8 0.3 collective-permute-start.7
  29.1 2.7 %visit.14 = (f32[80,768]{1,0:T(8,128)S(1)}, f32[80,768]{1,0:T(8,128)S(1)}) custom-call(f32[64,768]{1,0:T(8,128)S(1)} %collective-permute-done.6.refs_0_, bf16[144,768]{1,0:T(8,128)(2,1)S(1)} %get-tuple-element.41.refs_1_, bf16[128,768]{1,0:T(8,128)(2,1)S(1)} %get-tuple-element.42.refs_2_, ...), custom_call_target="tpu_custom_call", output_to_operand_aliasing={{0}: (5, {}), {1}: (6, {})} | custom-call | flops 2000000000 | bytes 1000000 | tf_op jit(solution)/shard_map/visit/pallas_call | solution.py:186
  32.0 2.7 %visit.15 = (f32[80,768]{1,0:T(8,128)S(1)}, f32[80,768]{1,0:T(8,128)S(1)}) custom-call(f32[64,768]{1,0:T(8,128)S(1)} %collective-permute-done.3.refs_0_, bf16[144,768]{1,0:T(8,128)(2,1)S(1)} %get-tuple-element.41.refs_1_, bf16[128,768]{1,0:T(8,128)(2,1)S(1)} %get-tuple-element.42.refs_2_, ...), custom_call_target="tpu_custom_call", output_to_operand_aliasing={{0}: (5, {}), {1}: (6, {})} | custom-call | flops 2000000000 | bytes 1000000 | tf_op jit(solution)/shard_map/visit/pallas_call | solution.py:186
  34.7 0.2 collective-permute-done.7.refs_0_
  34.8 0.5 %collective-permute-start.8 = (f32[64,768]{1,0:T(8,128)S(1)}, f32[64,768]{1,0:T(8,128)S(1)}, u32[]{:S(2)}, u32[]{:S(2)}) collective-permute-start(f32[64,768]{1,0:T(8,128)S(1)} %collective-permute-done.7.refs_0_), channel_id=1, source_target_pairs={{0,30},{1,3},{2,0},{3,5},{4,2},{5,7},{6,4},{7,9},{8,6},{9,11},{10,... | collective-permute-start | bytes 589832 | tf_op jit(solution)/shard_map/ppermute | solution.py:248
  35.4 2.7 %visit.16 = (f32[80,768]{1,0:T(8,128)S(1)}, f32[80,768]{1,0:T(8,128)S(1)}) custom-call(f32[64,768]{1,0:T(8,128)S(1)} %collective-permute-done.7.refs_0_, bf16[144,768]{1,0:T(8,128)(2,1)S(1)} %get-tuple-element.41.refs_1_, bf16[128,768]{1,0:T(8,128)(2,1)S(1)} %get-tuple-element.42.refs_2_, ...), custom_call_target="tpu_custom_call", output_to_operand_aliasing={{0}: (5, {}), {1}: (6, {})} | custom-call | flops 2000000000 | bytes 1000000 | tf_op jit(solution)/shard_map/visit/pallas_call | solution.py:186
  38.1 1.6 %visit.18.refs_3_ = f32[80,768]{1,0:T(8,128)S(1)} custom-call(f32[64,768]{1,0:T(8,128)S(1)} %collective-permute-done.4.refs_0_, bf16[144,768]{1,0:T(8,128)(2,1)S(1)} %get-tuple-element.47.refs_3_.refs_1_, bf16[128,768]{1,0:T(8,128)(2,1)S(1)} %get-tuple-element.48.refs_4_.refs_2_, f32[80,768]{1,0:T(8,128)S(1)} %get-tuple-element.71.refs_3_), custom_call_target="tpu_custom_call", output_to_operand_aliasing={{}: (3, {})} | custom-call | flops 1000000000 | bytes 1000000 | tf_op jit(solution)/shard_map/visit/pallas_call | solution.py:186
  39.6 0.9 %collective-permute-done.8.refs_0_ = f32[64,768]{1,0:T(8,128)S(1)} collective-permute-done((f32[64,768]{1,0:T(8,128)S(1)}, f32[64,768]{1,0:T(8,128)S(1)}, u32[]{:S(2)}, u32[]{:S(2)}) %collective-permute-start.8) | collective-permute-done | bytes 196640 | tf_op jit(solution)/shard_map/ppermute | solution.py:248
  40.6 1.6 %visit.19 = (f32[80,768]{1,0:T(8,128)S(1)}, f32[32,768]{1,0:T(8,128)S(1)}) custom-call(f32[64,768]{1,0:T(8,128)S(1)} %collective-permute-done.8.refs_0_, bf16[144,768]{1,0:T(8,128)(2,1)S(1)} %get-tuple-element.47.refs_3_.refs_1_, bf16[128,768]{1,0:T(8,128)(2,1)S(1)} %get-tuple-element.48.refs_4_.refs_2_, ...), custom_call_target="tpu_custom_call", output_to_operand_aliasing={{0}: (3, {})} | custom-call | flops 1000000000 | bytes 1000000 | tf_op jit(solution)/shard_map/visit/pallas_call | solution.py:186
  42.1 6.7 %collective-permute-start.9 = (f32[32,768]{1,0:T(8,128)S(1)}, f32[32,768]{1,0:T(8,128)S(1)}, u32[]{:S(2)}, u32[]{:S(2)}) collective-permute-start(f32[32,768]{1,0:T(8,128)S(1)} %get-tuple-element.74), channel_id=1, source_target_pairs={{0,1},{1,0},{2,3},{3,2},{4,5},{5,4},{6,7},{7,6},{8,9},{9,8},{10,11... | collective-permute-start | bytes 294920 | tf_op jit(solution)/shard_map/ppermute | solution.py:242
  48.8 1.6 %visit.17 = (f32[80,768]{1,0:T(8,128)S(1)}, f32[32,768]{1,0:T(8,128)S(1)}) custom-call(f32[64,768]{1,0:T(8,128)S(1)} %collective-permute-done.4.refs_0_, bf16[144,768]{1,0:T(8,128)(2,1)S(1)} %get-tuple-element.41.refs_1_, bf16[128,768]{1,0:T(8,128)(2,1)S(1)} %get-tuple-element.42.refs_2_, ...), custom_call_target="tpu_custom_call", output_to_operand_aliasing={{0}: (3, {})} | custom-call | flops 1000000000 | bytes 1000000 | tf_op jit(solution)/shard_map/visit/pallas_call | solution.py:186
  50.4 0.7 %add_multiply_fusion = f32[32,768]{1,0:T(8,128)} fusion(f32[32,768]{1,0:T(8,128)S(1)} %get-tuple-element.70, f32[32,768]{1,0:T(8,128)S(1)} %collective-permute-done.9, f32[32]{0:T(128)S(1)} %broadcast_divide_fusion), kind=kLoop, calls=%fused_computation | loop fusion | flops 49152 | bytes 295040 | tf_op jit(solution)/shard_map/mul | solution.py:275
  (18 shorter events, 0.5 us)
Async XLA Ops:
  0.0 0.9 %copy-start = (f32[15,768]{1,0:T(8,128)S(1)}, f32[15,768]{1,0:T(8,128)}, u32[]{:S(2)}) copy-start(f32[15,768]{1,0:T(8,128)} %solves.1) | copy-start | bytes 138244
  0.0 1.0 %copy-start.1 = (f32[15,768]{1,0:T(8,128)S(1)}, f32[15,768]{1,0:T(8,128)}, u32[]{:S(2)}) copy-start(f32[15,768]{1,0:T(8,128)} %probes.1) | copy-start | bytes 138244
  0.0 1.0 %copy-start.2 = (f32[768]{0:T(1024)S(1)}, f32[768]{0:T(1024)}, u32[]{:S(2)}) copy-start(f32[768]{0:T(1024)} %param.6) | copy-start | bytes 9220
  0.9 0.7 %copy-start.3 = (f32[32]{0:T(128)S(1)}, f32[32]{0:T(128)}, u32[]{:S(2)}) copy-start(f32[32]{0:T(128)} %param.9) | copy-start | bytes 388
  1.7 11.1 %collective-permute-start.1 = (f32[64,768]{1,0:T(8,128)S(1)}, f32[64,768]{1,0:T(8,128)S(1)}, u32[]{:S(2)}, u32[]{:S(2)}) collective-permute-start(f32[64,768]{1,0:T(8,128)S(1)} %get-tuple-element.46.refs_4_), channel_id=1, source_target_pairs={{0,1},{1,0},{2,3},{3,2},{4,5},{5,4},{6,7},{7,6},{8,9},{9,8},{10,11... | collective-permute-start | bytes 589832 | tf_op jit(solution)/shard_map/ppermute | solution.py:242
  11.8 6.8 %collective-permute-start = (f32[64,768]{1,0:T(8,128)S(1)}, f32[64,768]{1,0:T(8,128)S(1)}, u32[]{:S(2)}, u32[]{:S(2)}) collective-permute-start(f32[64,768]{1,0:T(8,128)S(1)} %get-tuple-element.46.refs_4_), channel_id=1, source_target_pairs={{0,30},{1,3},{2,0},{3,5},{4,2},{5,7},{6,4},{7,9},{8,6},{9,11},{10,... | collective-permute-start | bytes 589832 | tf_op jit(solution)/shard_map/ppermute | solution.py:248
  14.4 7.5 %collective-permute-start.5 = (f32[64,768]{1,0:T(8,128)S(1)}, f32[64,768]{1,0:T(8,128)S(1)}, u32[]{:S(2)}, u32[]{:S(2)}) collective-permute-start(f32[64,768]{1,0:T(8,128)S(1)} %get-tuple-element.46.refs_4_), channel_id=1, source_target_pairs={{0,3},{1,30},{2,5},{3,0},{4,7},{5,2},{6,9},{7,4},{8,11},{9,6},{10,... | collective-permute-start | bytes 589832 | tf_op jit(solution)/shard_map/ppermute | solution.py:248
  18.6 7.4 %collective-permute-start.2 = (f32[64,768]{1,0:T(8,128)S(1)}, f32[64,768]{1,0:T(8,128)S(1)}, u32[]{:S(2)}, u32[]{:S(2)}) collective-permute-start(f32[64,768]{1,0:T(8,128)S(1)} %collective-permute-done.refs_0_), channel_id=1, source_target_pairs={{0,30},{1,3},{2,0},{3,5},{4,2},{5,7},{6,4},{7,9},{8,6},{9,11},{10,... | collective-permute-start | bytes 589832 | tf_op jit(solution)/shard_map/ppermute | solution.py:248
  21.9 6.9 %collective-permute-start.6 = (f32[64,768]{1,0:T(8,128)S(1)}, f32[64,768]{1,0:T(8,128)S(1)}, u32[]{:S(2)}, u32[]{:S(2)}) collective-permute-start(f32[64,768]{1,0:T(8,128)S(1)} %collective-permute-done.5.refs_0_), channel_id=1, source_target_pairs={{0,30},{1,3},{2,0},{3,5},{4,2},{5,7},{6,4},{7,9},{8,6},{9,11},{10,... | collective-permute-start | bytes 589832 | tf_op jit(solution)/shard_map/ppermute | solution.py:248
  26.0 5.9 %collective-permute-start.3 = (f32[64,768]{1,0:T(8,128)S(1)}, f32[64,768]{1,0:T(8,128)S(1)}, u32[]{:S(2)}, u32[]{:S(2)}) collective-permute-start(f32[64,768]{1,0:T(8,128)S(1)} %collective-permute-done.2.refs_0_), channel_id=1, source_target_pairs={{0,30},{1,3},{2,0},{3,5},{4,2},{5,7},{6,4},{7,9},{8,6},{9,11},{10,... | collective-permute-start | bytes 589832 | tf_op jit(solution)/shard_map/ppermute | solution.py:248
  28.8 6.0 %collective-permute-start.7 = (f32[64,768]{1,0:T(8,128)S(1)}, f32[64,768]{1,0:T(8,128)S(1)}, u32[]{:S(2)}, u32[]{:S(2)}) collective-permute-start(f32[64,768]{1,0:T(8,128)S(1)} %collective-permute-done.6.refs_0_), channel_id=1, source_target_pairs={{0,30},{1,3},{2,0},{3,5},{4,2},{5,7},{6,4},{7,9},{8,6},{9,11},{10,... | collective-permute-start | bytes 589832 | tf_op jit(solution)/shard_map/ppermute | solution.py:248
  31.8 6.2 %collective-permute-start.4 = (f32[64,768]{1,0:T(8,128)S(1)}, f32[64,768]{1,0:T(8,128)S(1)}, u32[]{:S(2)}, u32[]{:S(2)}) collective-permute-start(f32[64,768]{1,0:T(8,128)S(1)} %collective-permute-done.3.refs_0_), channel_id=1, source_target_pairs={{0,30},{1,3},{2,0},{3,5},{4,2},{5,7},{6,4},{7,9},{8,6},{9,11},{10,... | collective-permute-start | bytes 589832 | tf_op jit(solution)/shard_map/ppermute | solution.py:248
  34.8 5.7 %collective-permute-start.8 = (f32[64,768]{1,0:T(8,128)S(1)}, f32[64,768]{1,0:T(8,128)S(1)}, u32[]{:S(2)}, u32[]{:S(2)}) collective-permute-start(f32[64,768]{1,0:T(8,128)S(1)} %collective-permute-done.7.refs_0_), channel_id=1, source_target_pairs={{0,30},{1,3},{2,0},{3,5},{4,2},{5,7},{6,4},{7,9},{8,6},{9,11},{10,... | collective-permute-start | bytes 589832 | tf_op jit(solution)/shard_map/ppermute | solution.py:248
  42.1 8.3 %collective-permute-start.9 = (f32[32,768]{1,0:T(8,128)S(1)}, f32[32,768]{1,0:T(8,128)S(1)}, u32[]{:S(2)}, u32[]{:S(2)}) collective-permute-start(f32[32,768]{1,0:T(8,128)S(1)} %get-tuple-element.74), channel_id=1, source_target_pairs={{0,1},{1,0},{2,3},{3,2},{4,5},{5,4},{6,7},{7,6},{8,9},{9,8},{10,11... | collective-permute-start | bytes 294920 | tf_op jit(solution)/shard_map/ppermute | solution.py:242
where the time goes:
time: 51.3 us; the launch traced here: 51.2 us
  starting transfers between devices  23.7 us (46%)
  Pallas kernels  22.5 us (44%)
  waiting for transfers between devices  2.51 us (5%)
  other arithmetic  1.64 us (3%)
  local copies, waits for them, and re-layouts  0.63 us (1%)
    pallas_call x10, Pallas kernels, visit(): pl.pallas_call(functools.partial(visit_kernel, half_inv, pairs, len(vis),...  22.3 us
    ppermute x2, starting transfers between devices, swapped(): lax.ppermute(value, 'blk', [(b, b + 1 - 2 * (b % 2)) for b in range(count)])  16.7 us
    ppermute x8, starting transfers between devices, toward(): return lax.ppermute(value, 'blk', pairs)  6.99 us
    ppermute x8, waiting for transfers between devices, toward(): return lax.ppermute(value, 'blk', pairs)  1.44 us
    ppermute x2, waiting for transfers between devices, swapped(): lax.ppermute(value, 'blk', [(b, b + 1 - 2 * (b % 2)) for b in range(count)])  1.07 us
  transfers between devices with their start and end apart: 10, of which 5 were waited for; matrix products, arithmetic and copies ran while one was open for 0% of the time, Pallas kernels for 41%

commit v1 on v0

--- a/solution.py
+++ b/solution.py
@@ -12,7 +12,7 @@
 f32, bf16 = jnp.float32, jnp.bfloat16
 VMEM = pl.BlockSpec(memory_space=pltpu.VMEM)
 DIM, GROUP, SUMS = 32, 16, 80
-STEP, BACK, AHEAD, LAG = 128, 256, 1, 2
+STEP, BACK, AHEAD, LAG = 192, 192, 1, 1
 
 
 def halves(value):

time: 51.3 us -> 50.5 us (0.984)
  waiting for transfers between devices: 2.51 us -> 3.84 us
  Pallas kernels: 22.5 us -> 21.4 us
  starting transfers between devices: 23.7 us -> 22.7 us
    ppermute x8, waiting for transfers between devices: 1.44 us -> 2.77 us  [toward(): return lax.ppermute(value, 'blk', pairs)]
    pallas_call x10, Pallas kernels: 22.3 us -> 21.3 us  [visit(): pl.pallas_call(functools.partial(visit_kernel, half_inv, pairs, len(vis),...]
    ppermute x8, starting transfers between devices: 6.99 us -> 6.23 us  [toward(): return lax.ppermute(value, 'blk', pairs)]
  transfers between devices with their start and end apart: 10 -> 10, of which waited for: 5 -> 7; matrix products, arithmetic and copies ran while one was open for 0% -> 0% of each run, Pallas kernels for 41% -> 39%
where the time goes in v1:
time: 50.5 us; the launch traced here: 50.4 us
  starting transfers between devices  22.7 us (45%)
  Pallas kernels  21.4 us (42%)
  waiting for transfers between devices  3.84 us (8%)
  other arithmetic  1.64 us (3%)
  local copies, waits for them, and re-layouts  0.63 us (1%)
    pallas_call x10, Pallas kernels, visit(): pl.pallas_call(functools.partial(visit_kernel, half_inv, pairs, len(vis),...  21.3 us
    ppermute x2, starting transfers between devices, swapped(): lax.ppermute(value, 'blk', [(b, b + 1 - 2 * (b % 2)) for b in range(count)])  16.4 us
    ppermute x8, starting transfers between devices, toward(): return lax.ppermute(value, 'blk', pairs)  6.23 us
    ppermute x8, waiting for transfers between devices, toward(): return lax.ppermute(value, 'blk', pairs)  2.77 us
    ppermute x2, waiting for transfers between devices, swapped(): lax.ppermute(value, 'blk', [(b, b + 1 - 2 * (b % 2)) for b in range(count)])  1.07 us
  transfers between devices with their start and end apart: 10, of which 7 were waited for; matrix products, arithmetic and copies ran while one was open for 0% of the time, Pallas kernels for 39%

profile of v1, /device:TPU:69, one launch (start us, length us, event | category | flops | bytes accessed | tf_op | source)
XLA Modules:
  0.0 50.4 jit_solution(15772367505899710805)
XLA Ops:
  0.0 0.9 %broadcast_multiply_fusion.coords = f32[32,768]{1,0:T(8,128)S(1)} fusion(f32[32,768]{1,0:T(8,128)} %param.5), kind=kLoop, calls=%fused_computation.1 | loop fusion | flops 24576 | bytes 196608 | tf_op jit(solution)/shard_map/mul | solution.py:225
  1.0 0.6 %copy-done.3 = f32[32]{0:T(128)S(1)} copy-done((f32[32]{0:T(128)S(1)}, f32[32]{0:T(128)}, u32[]{:S(2)}) %copy-start.3) | copy-done | bytes 152
  1.7 10.0 %collective-permute-start.1 = (f32[64,768]{1,0:T(8,128)S(1)}, f32[64,768]{1,0:T(8,128)S(1)}, u32[]{:S(2)}, u32[]{:S(2)}) collective-permute-start(f32[64,768]{1,0:T(8,128)S(1)} %get-tuple-element.46.refs_4_), channel_id=1, source_target_pairs={{0,1},{1,0},{2,3},{3,2},{4,5},{5,4},{6,7},{7,6},{8,9},{9,8},{10,11... | collective-permute-start | bytes 589832 | tf_op jit(solution)/shard_map/ppermute | solution.py:242
  11.8 1.1 %collective-permute-done.1.refs_0_.refs_4_ = f32[64,768]{1,0:T(8,128)S(1)} collective-permute-done((f32[64,768]{1,0:T(8,128)S(1)}, f32[64,768]{1,0:T(8,128)S(1)}, u32[]{:S(2)}, u32[]{:S(2)}) %collective-permute-start.1) | collective-permute-done | bytes 196640 | tf_op jit(solution)/shard_map/ppermute | solution.py:242
  12.8 1.4 %visit.10 = (f32[80,768]{1,0:T(8,128)S(1)}, bf16[144,768]{1,0:T(8,128)(2,1)S(1)}, bf16[128,768]{1,0:T(8,128)(2,1)S(1)}) custom-call(f32[64,768]{1,0:T(8,128)S(1)} %collective-permute-done.1.refs_0_.refs_4_, bf16[144,768]{1,0:T(8,128)(2,1)S(1)} %get-tuple-element.41.refs_1_, bf16[128,768]{1,0:T(8,128)(2,1)S(1)} %get-tuple-element.42.refs_2_), custom_call_target="tpu_custom_call" | custom-call | flops 1000000000 | bytes 1000000 | tf_op jit(solution)/shard_map/visit/pallas_call | solution.py:186
  14.3 4.2 %collective-permute-start.5 = (f32[64,768]{1,0:T(8,128)S(1)}, f32[64,768]{1,0:T(8,128)S(1)}, u32[]{:S(2)}, u32[]{:S(2)}) collective-permute-start(f32[64,768]{1,0:T(8,128)S(1)} %get-tuple-element.46.refs_4_), channel_id=1, source_target_pairs={{0,3},{1,30},{2,5},{3,0},{4,7},{5,2},{6,9},{7,4},{8,11},{9,6},{10,... | collective-permute-start | bytes 589832 | tf_op jit(solution)/shard_map/ppermute | solution.py:248
  18.6 0.3 collective-permute-start.2
  18.9 2.5 %visit.11 = (f32[80,768]{1,0:T(8,128)S(1)}, f32[80,768]{1,0:T(8,128)S(1)}) custom-call(f32[64,768]{1,0:T(8,128)S(1)} %collective-permute-done.refs_0_, bf16[144,768]{1,0:T(8,128)(2,1)S(1)} %get-tuple-element.41.refs_1_, bf16[128,768]{1,0:T(8,128)(2,1)S(1)} %get-tuple-element.42.refs_2_, ...), custom_call_target="tpu_custom_call", output_to_operand_aliasing={{0}: (5, {})} | custom-call | flops 2000000000 | bytes 1000000 | tf_op jit(solution)/shard_map/visit/pallas_call | solution.py:186
  21.4 0.4 collective-permute-done.5.refs_0_
  21.8 1.4 %collective-permute-start.6 = (f32[64,768]{1,0:T(8,128)S(1)}, f32[64,768]{1,0:T(8,128)S(1)}, u32[]{:S(2)}, u32[]{:S(2)}) collective-permute-start(f32[64,768]{1,0:T(8,128)S(1)} %collective-permute-done.5.refs_0_), channel_id=1, source_target_pairs={{0,30},{1,3},{2,0},{3,5},{4,2},{5,7},{6,4},{7,9},{8,6},{9,11},{10,... | collective-permute-start | bytes 589832 | tf_op jit(solution)/shard_map/ppermute | solution.py:248
  23.2 2.6 %visit.12 = (f32[80,768]{1,0:T(8,128)S(1)}, f32[80,768]{1,0:T(8,128)S(1)}) custom-call(f32[64,768]{1,0:T(8,128)S(1)} %collective-permute-done.5.refs_0_, bf16[144,768]{1,0:T(8,128)(2,1)S(1)} %get-tuple-element.41.refs_1_, bf16[128,768]{1,0:T(8,128)(2,1)S(1)} %get-tuple-element.42.refs_2_, ...), custom_call_target="tpu_custom_call", output_to_operand_aliasing={{0}: (5, {}), {1}: (6, {})} | custom-call | flops 2000000000 | bytes 1000000 | tf_op jit(solution)/shard_map/visit/pallas_call | solution.py:186
  25.9 2.6 %visit.13 = (f32[80,768]{1,0:T(8,128)S(1)}, f32[80,768]{1,0:T(8,128)S(1)}) custom-call(f32[64,768]{1,0:T(8,128)S(1)} %collective-permute-done.2.refs_0_, bf16[144,768]{1,0:T(8,128)(2,1)S(1)} %get-tuple-element.41.refs_1_, bf16[128,768]{1,0:T(8,128)(2,1)S(1)} %get-tuple-element.42.refs_2_, ...), custom_call_target="tpu_custom_call", output_to_operand_aliasing={{0}: (5, {}), {1}: (6, {})} | custom-call | flops 2000000000 | bytes 1000000 | tf_op jit(solution)/shard_map/visit/pallas_call | solution.py:186
  28.5 0.3 collective-permute-start.7
  28.8 2.6 %visit.14 = (f32[80,768]{1,0:T(8,128)S(1)}, f32[80,768]{1,0:T(8,128)S(1)}) custom-call(f32[64,768]{1,0:T(8,128)S(1)} %collective-permute-done.6.refs_0_, bf16[144,768]{1,0:T(8,128)(2,1)S(1)} %get-tuple-element.41.refs_1_, bf16[128,768]{1,0:T(8,128)(2,1)S(1)} %get-tuple-element.42.refs_2_, ...), custom_call_target="tpu_custom_call", output_to_operand_aliasing={{0}: (5, {}), {1}: (6, {})} | custom-call | flops 2000000000 | bytes 1000000 | tf_op jit(solution)/shard_map/visit/pallas_call | solution.py:186
  31.6 2.6 %visit.15 = (f32[80,768]{1,0:T(8,128)S(1)}, f32[80,768]{1,0:T(8,128)S(1)}) custom-call(f32[64,768]{1,0:T(8,128)S(1)} %collective-permute-done.3.refs_0_, bf16[144,768]{1,0:T(8,128)(2,1)S(1)} %get-tuple-element.41.refs_1_, bf16[128,768]{1,0:T(8,128)(2,1)S(1)} %get-tuple-element.42.refs_2_, ...), custom_call_target="tpu_custom_call", output_to_operand_aliasing={{0}: (5, {}), {1}: (6, {})} | custom-call | flops 2000000000 | bytes 1000000 | tf_op jit(solution)/shard_map/visit/pallas_call | solution.py:186
  34.2 0.3 collective-permute-done.7.refs_0_
  34.5 2.6 %visit.16 = (f32[80,768]{1,0:T(8,128)S(1)}, f32[80,768]{1,0:T(8,128)S(1)}) custom-call(f32[64,768]{1,0:T(8,128)S(1)} %collective-permute-done.7.refs_0_, bf16[144,768]{1,0:T(8,128)(2,1)S(1)} %get-tuple-element.41.refs_1_, bf16[128,768]{1,0:T(8,128)(2,1)S(1)} %get-tuple-element.42.refs_2_, ...), custom_call_target="tpu_custom_call", output_to_operand_aliasing={{0}: (5, {}), {1}: (6, {})} | custom-call | flops 2000000000 | bytes 1000000 | tf_op jit(solution)/shard_map/visit/pallas_call | solution.py:186
  37.1 0.2 collective-permute-done.4.refs_0_
  37.3 1.5 %visit.18.refs_3_ = f32[80,768]{1,0:T(8,128)S(1)} custom-call(f32[64,768]{1,0:T(8,128)S(1)} %collective-permute-done.4.refs_0_, bf16[144,768]{1,0:T(8,128)(2,1)S(1)} %get-tuple-element.47.refs_3_.refs_1_, bf16[128,768]{1,0:T(8,128)(2,1)S(1)} %get-tuple-element.48.refs_4_.refs_2_, f32[80,768]{1,0:T(8,128)S(1)} %get-tuple-element.71.refs_3_), custom_call_target="tpu_custom_call", output_to_operand_aliasing={{}: (3, {})} | custom-call | flops 1000000000 | bytes 1000000 | tf_op jit(solution)/shard_map/visit/pallas_call | solution.py:186
  38.8 1.4 %collective-permute-done.8.refs_0_ = f32[64,768]{1,0:T(8,128)S(1)} collective-permute-done((f32[64,768]{1,0:T(8,128)S(1)}, f32[64,768]{1,0:T(8,128)S(1)}, u32[]{:S(2)}, u32[]{:S(2)}) %collective-permute-start.8) | collective-permute-done | bytes 196640 | tf_op jit(solution)/shard_map/ppermute | solution.py:248
  40.2 1.5 %visit.19 = (f32[80,768]{1,0:T(8,128)S(1)}, f32[32,768]{1,0:T(8,128)S(1)}) custom-call(f32[64,768]{1,0:T(8,128)S(1)} %collective-permute-done.8.refs_0_, bf16[144,768]{1,0:T(8,128)(2,1)S(1)} %get-tuple-element.47.refs_3_.refs_1_, bf16[128,768]{1,0:T(8,128)(2,1)S(1)} %get-tuple-element.48.refs_4_.refs_2_, ...), custom_call_target="tpu_custom_call", output_to_operand_aliasing={{0}: (3, {})} | custom-call | flops 1000000000 | bytes 1000000 | tf_op jit(solution)/shard_map/visit/pallas_call | solution.py:186
  41.7 6.4 %collective-permute-start.9 = (f32[32,768]{1,0:T(8,128)S(1)}, f32[32,768]{1,0:T(8,128)S(1)}, u32[]{:S(2)}, u32[]{:S(2)}) collective-permute-start(f32[32,768]{1,0:T(8,128)S(1)} %get-tuple-element.74), channel_id=1, source_target_pairs={{0,1},{1,0},{2,3},{3,2},{4,5},{5,4},{6,7},{7,6},{8,9},{9,8},{10,11... | collective-permute-start | bytes 294920 | tf_op jit(solution)/shard_map/ppermute | solution.py:242
  48.2 1.5 %visit.17 = (f32[80,768]{1,0:T(8,128)S(1)}, f32[32,768]{1,0:T(8,128)S(1)}) custom-call(f32[64,768]{1,0:T(8,128)S(1)} %collective-permute-done.4.refs_0_, bf16[144,768]{1,0:T(8,128)(2,1)S(1)} %get-tuple-element.41.refs_1_, bf16[128,768]{1,0:T(8,128)(2,1)S(1)} %get-tuple-element.42.refs_2_, ...), custom_call_target="tpu_custom_call", output_to_operand_aliasing={{0}: (3, {})} | custom-call | flops 1000000000 | bytes 1000000 | tf_op jit(solution)/shard_map/visit/pallas_call | solution.py:186
  49.7 0.7 %add_multiply_fusion = f32[32,768]{1,0:T(8,128)} fusion(f32[32,768]{1,0:T(8,128)S(1)} %get-tuple-element.70, f32[32,768]{1,0:T(8,128)S(1)} %collective-permute-done.9, f32[32]{0:T(128)S(1)} %broadcast_divide_fusion), kind=kLoop, calls=%fused_computation | loop fusion | flops 49152 | bytes 295040 | tf_op jit(solution)/shard_map/mul | solution.py:275
  (18 shorter events, 0.7 us)
Async XLA Ops:
  0.0 0.9 %copy-start = (f32[15,768]{1,0:T(8,128)S(1)}, f32[15,768]{1,0:T(8,128)}, u32[]{:S(2)}) copy-start(f32[15,768]{1,0:T(8,128)} %solves.1) | copy-start | bytes 138244
  0.0 1.0 %copy-start.1 = (f32[15,768]{1,0:T(8,128)S(1)}, f32[15,768]{1,0:T(8,128)}, u32[]{:S(2)}) copy-start(f32[15,768]{1,0:T(8,128)} %probes.1) | copy-start | bytes 138244
  0.0 1.0 %copy-start.2 = (f32[768]{0:T(1024)S(1)}, f32[768]{0:T(1024)}, u32[]{:S(2)}) copy-start(f32[768]{0:T(1024)} %param.6) | copy-start | bytes 9220
  0.9 0.7 %copy-start.3 = (f32[32]{0:T(128)S(1)}, f32[32]{0:T(128)}, u32[]{:S(2)}) copy-start(f32[32]{0:T(128)} %param.9) | copy-start | bytes 388
  1.7 11.1 %collective-permute-start.1 = (f32[64,768]{1,0:T(8,128)S(1)}, f32[64,768]{1,0:T(8,128)S(1)}, u32[]{:S(2)}, u32[]{:S(2)}) collective-permute-start(f32[64,768]{1,0:T(8,128)S(1)} %get-tuple-element.46.refs_4_), channel_id=1, source_target_pairs={{0,1},{1,0},{2,3},{3,2},{4,5},{5,4},{6,7},{7,6},{8,9},{9,8},{10,11... | collective-permute-start | bytes 589832 | tf_op jit(solution)/shard_map/ppermute | solution.py:242
  11.8 6.8 %collective-permute-start = (f32[64,768]{1,0:T(8,128)S(1)}, f32[64,768]{1,0:T(8,128)S(1)}, u32[]{:S(2)}, u32[]{:S(2)}) collective-permute-start(f32[64,768]{1,0:T(8,128)S(1)} %get-tuple-element.46.refs_4_), channel_id=1, source_target_pairs={{0,30},{1,3},{2,0},{3,5},{4,2},{5,7},{6,4},{7,9},{8,6},{9,11},{10,... | collective-permute-start | bytes 589832 | tf_op jit(solution)/shard_map/ppermute | solution.py:248
  14.3 7.5 %collective-permute-start.5 = (f32[64,768]{1,0:T(8,128)S(1)}, f32[64,768]{1,0:T(8,128)S(1)}, u32[]{:S(2)}, u32[]{:S(2)}) collective-permute-start(f32[64,768]{1,0:T(8,128)S(1)} %get-tuple-element.46.refs_4_), channel_id=1, source_target_pairs={{0,3},{1,30},{2,5},{3,0},{4,7},{5,2},{6,9},{7,4},{8,11},{9,6},{10,... | collective-permute-start | bytes 589832 | tf_op jit(solution)/shard_map/ppermute | solution.py:248
  18.6 7.2 %collective-permute-start.2 = (f32[64,768]{1,0:T(8,128)S(1)}, f32[64,768]{1,0:T(8,128)S(1)}, u32[]{:S(2)}, u32[]{:S(2)}) collective-permute-start(f32[64,768]{1,0:T(8,128)S(1)} %collective-permute-done.refs_0_), channel_id=1, source_target_pairs={{0,30},{1,3},{2,0},{3,5},{4,2},{5,7},{6,4},{7,9},{8,6},{9,11},{10,... | collective-permute-start | bytes 589832 | tf_op jit(solution)/shard_map/ppermute | solution.py:248
  21.8 6.7 %collective-permute-start.6 = (f32[64,768]{1,0:T(8,128)S(1)}, f32[64,768]{1,0:T(8,128)S(1)}, u32[]{:S(2)}, u32[]{:S(2)}) collective-permute-start(f32[64,768]{1,0:T(8,128)S(1)} %collective-permute-done.5.refs_0_), channel_id=1, source_target_pairs={{0,30},{1,3},{2,0},{3,5},{4,2},{5,7},{6,4},{7,9},{8,6},{9,11},{10,... | collective-permute-start | bytes 589832 | tf_op jit(solution)/shard_map/ppermute | solution.py:248
  25.8 5.8 %collective-permute-start.3 = (f32[64,768]{1,0:T(8,128)S(1)}, f32[64,768]{1,0:T(8,128)S(1)}, u32[]{:S(2)}, u32[]{:S(2)}) collective-permute-start(f32[64,768]{1,0:T(8,128)S(1)} %collective-permute-done.2.refs_0_), channel_id=1, source_target_pairs={{0,30},{1,3},{2,0},{3,5},{4,2},{5,7},{6,4},{7,9},{8,6},{9,11},{10,... | collective-permute-start | bytes 589832 | tf_op jit(solution)/shard_map/ppermute | solution.py:248
  28.5 6.0 %collective-permute-start.7 = (f32[64,768]{1,0:T(8,128)S(1)}, f32[64,768]{1,0:T(8,128)S(1)}, u32[]{:S(2)}, u32[]{:S(2)}) collective-permute-start(f32[64,768]{1,0:T(8,128)S(1)} %collective-permute-done.6.refs_0_), channel_id=1, source_target_pairs={{0,30},{1,3},{2,0},{3,5},{4,2},{5,7},{6,4},{7,9},{8,6},{9,11},{10,... | collective-permute-start | bytes 589832 | tf_op jit(solution)/shard_map/ppermute | solution.py:248
  31.6 5.7 %collective-permute-start.4 = (f32[64,768]{1,0:T(8,128)S(1)}, f32[64,768]{1,0:T(8,128)S(1)}, u32[]{:S(2)}, u32[]{:S(2)}) collective-permute-start(f32[64,768]{1,0:T(8,128)S(1)} %collective-permute-done.3.refs_0_), channel_id=1, source_target_pairs={{0,30},{1,3},{2,0},{3,5},{4,2},{5,7},{6,4},{7,9},{8,6},{9,11},{10,... | collective-permute-start | bytes 589832 | tf_op jit(solution)/shard_map/ppermute | solution.py:248
  34.5 5.7 %collective-permute-start.8 = (f32[64,768]{1,0:T(8,128)S(1)}, f32[64,768]{1,0:T(8,128)S(1)}, u32[]{:S(2)}, u32[]{:S(2)}) collective-permute-start(f32[64,768]{1,0:T(8,128)S(1)} %collective-permute-done.7.refs_0_), channel_id=1, source_target_pairs={{0,30},{1,3},{2,0},{3,5},{4,2},{5,7},{6,4},{7,9},{8,6},{9,11},{10,... | collective-permute-start | bytes 589832 | tf_op jit(solution)/shard_map/ppermute | solution.py:248
  41.7 7.9 %collective-permute-start.9 = (f32[32,768]{1,0:T(8,128)S(1)}, f32[32,768]{1,0:T(8,128)S(1)}, u32[]{:S(2)}, u32[]{:S(2)}) collective-permute-start(f32[32,768]{1,0:T(8,128)S(1)} %get-tuple-element.74), channel_id=1, source_target_pairs={{0,1},{1,0},{2,3},{3,2},{4,5},{5,4},{6,7},{7,6},{8,9},{9,8},{10,11... | collective-permute-start | bytes 294920 | tf_op jit(solution)/shard_map/ppermute | solution.py:242

commit v2 on v1

--- a/solution.py
+++ b/solution.py
@@ -35,22 +35,28 @@
     return edge.astype(bf16)
 
 
-def own_forms(field, dist_ref, coup_ref):
-    high, low = halves(field[:DIM])
+def scaled_halves(field, scale):
+    wide = jnp.concatenate([scale] * (field.shape[1] // scale.shape[1]), 1)
+    high, low = halves(field[:DIM] * wide)
+    return high, low, high.astype(f32) + low.astype(f32)
+
+
+def own_forms(field, scale, dist_ref, coup_ref):
+    high, low, near = scaled_halves(field, scale)
     first, second = field[DIM : DIM + GROUP], field[DIM + GROUP :]
-    square = jnp.broadcast_to(second[:1], first.shape)
+    square = jnp.broadcast_to(jnp.sum(near * near, 0, keepdims=True), first.shape)
     dist_ref[...] = jnp.concatenate([high, low, high, low, edge_rows(square, 3, 0)], 0)
     table = jnp.concatenate([row_is(0, first, second), row_is(0, 0.0, first)], 0)
     high, low = halves(table)
     coup_ref[...] = jnp.concatenate([high, low, high, low], 0)
 
 
-def visit_forms(half_inv, field, dist_ref, coup_ref, sums_ref):
+def visit_forms(half_inv, field, scale, dist_ref, coup_ref, sums_ref):
     points = field.shape[1]
-    high, low = halves(field[:DIM])
+    high, low, near = scaled_halves(field, scale)
     first, second = field[DIM : DIM + GROUP], field[DIM + GROUP :]
     sums_ref[...] = jnp.concatenate([high, low, jnp.ones((GROUP, points), bf16)], 0)
-    square = jnp.broadcast_to(second[:1], first.shape)
+    square = jnp.broadcast_to(jnp.sum(near * near, 0, keepdims=True), first.shape)
     twice = [-2.0 * high, -2.0 * low]
     zero = jnp.zeros((256 - 4 * DIM - GROUP, points), bf16)
     dist = jnp.concatenate([*twice, *twice[::-1], edge_rows(square, 0, 3), zero], 0)
@@ -126,9 +132,8 @@
             back(chunks[first], slot_of(first))
 
 
-def finish(field, acc):
-    high, low = halves(field[:DIM])
-    near = high.astype(f32) + low.astype(f32)
+def finish(field, scale, acc):
+    near = scaled_halves(field, scale)[2]
     return near * acc[2 * DIM : 2 * DIM + 1] - (acc[:DIM] + acc[DIM : 2 * DIM])
 
 
@@ -139,6 +144,7 @@
         taken, refs[:] = refs[:count], refs[count:]
         return taken
 
+    (scale,) = take(1)
     vis = take(n_vis)
     own = [take(2) for _ in range(n_own)]
     acc_in = take(n_acc)
@@ -153,18 +159,18 @@
         else:
             acc_out[index][...] = jnp.zeros_like(acc_out[index])
     for index in range(n_form):
-        own_forms(vis[index][...], *forms[index])
+        own_forms(vis[index][...], scale[...], *forms[index])
     sides = []
     for ref in vis:
         side = take(3)
-        visit_forms(half_inv, ref[...], *side)
+        visit_forms(half_inv, ref[...], scale[...], *side)
         sides.append(side)
     add_tiles(pairs, sides, own, acc_out, high_ref, low_ref)
     for o, field, out in zip(done, fields, outs):
-        out[...] = finish(field[...], acc_out[o][...])
-
-
-def visit(half_inv, pairs, vis, own, accs, n_form=0, done=(), fields=()):
+        out[...] = finish(field[...], scale[...], acc_out[o][...])
+
+
+def visit(half_inv, scale, pairs, vis, own, accs, n_form=0, done=(), fields=()):
     points = vis[0].shape[1]
     n_own = len(own)
     acc_shape = jax.ShapeDtypeStruct((SUMS, points), f32)
@@ -181,8 +187,8 @@
             pltpu.VMEM((points, 8 * GROUP), bf16),
             pltpu.VMEM((SUMS, points), bf16),
         ]
-    args = [*vis, *[ref for forms in own for ref in forms], *accs, *fields]
-    first = len(vis) + 2 * n_own
+    args = [scale, *vis, *[ref for forms in own for ref in forms], *accs, *fields]
+    first = 1 + len(vis) + 2 * n_own
     return pl.pallas_call(
         functools.partial(
             visit_kernel, half_inv, pairs, len(vis), n_own, len(accs), n_form, done
@@ -200,41 +206,55 @@
     )(*args)
 
 
-def field_kernel(coords, alpha, solves, probes, length, field, dist_ref, coup_ref):
+def field_kernel(coords, alpha, solves, probes, field):
+    middle = DIM + GROUP
+    lanes = alpha.shape[1]
+    field[0:DIM, :] = coords[...]
+    for index in range(alpha.shape[0]):
+        cols = slice(index * lanes, (index + 1) * lanes)
+        field[DIM : DIM + 1, cols] = alpha[index : index + 1, :]
+        field[middle : middle + 1, cols] = alpha[index : index + 1, :]
+    field[DIM + 1 : middle, :] = solves[...]
+    field[middle + 1 :, :] = probes[...]
+
+
+def make_field(coords, alpha, solves, probes):
+    args = (coords * root_five, alpha.reshape(-1, 128), solves, probes)
+    return pl.pallas_call(
+        field_kernel,
+        out_shape=jax.ShapeDtypeStruct((DIM + 2 * GROUP, coords.shape[1]), f32),
+        in_specs=[VMEM] * len(args),
+        out_specs=VMEM,
+        compiler_params=pltpu.CompilerParams(vmem_limit_bytes=8 * 2**20),
+        name="field",
+    )(*args)
+
+
+def scale_kernel(field, length, scale_ref, dist_ref, coup_ref):
     size = length.shape[1]
     spread = jnp.broadcast_to(length[...], (size, size))
     row = lax.broadcasted_iota(jnp.int32, (size, size), 0)
     col = lax.broadcasted_iota(jnp.int32, (size, size), 1)
     column = jnp.sum(jnp.where(row == col, spread, 0.0), 1, keepdims=True)
-    scaled = coords[...] * (1.0 / column)
-    high, low = halves(scaled)
-    near = high.astype(f32) + low.astype(f32)
-    middle = DIM + GROUP
-    lanes = alpha.shape[1]
-    field[0:DIM, :] = scaled
-    for index in range(alpha.shape[0]):
-        field[DIM : DIM + 1, index * lanes : (index + 1) * lanes] = alpha[index : index + 1, :]
-    field[DIM + 1 : middle, :] = solves[...]
-    field[middle : middle + 1, :] = jnp.sum(near * near, 0, keepdims=True)
-    field[middle + 1 :, :] = probes[...]
-    own_forms(field[...], dist_ref, coup_ref)
-
-
-def make_field(coords, alpha, solves, probes, lengthscale):
-    points = coords.shape[1]
-    args = (coords * root_five, alpha.reshape(-1, 128), solves, probes, lengthscale[None])
+    scale = jnp.broadcast_to(1.0 / column, scale_ref.shape)
+    scale_ref[...] = scale
+    own_forms(field[...], scale, dist_ref, coup_ref)
+
+
+def make_own(field, lengthscale):
+    points = field.shape[1]
     return pl.pallas_call(
-        field_kernel,
+        scale_kernel,
         out_shape=[
-            jax.ShapeDtypeStruct((DIM + 2 * GROUP, points), f32),
+            jax.ShapeDtypeStruct((DIM, 128), f32),
             jax.ShapeDtypeStruct((4 * DIM + GROUP, points), bf16),
             jax.ShapeDtypeStruct((8 * GROUP, points), bf16),
         ],
-        in_specs=[VMEM] * 5,
+        in_specs=[VMEM] * 2,
         out_specs=[VMEM] * 3,
         compiler_params=pltpu.CompilerParams(vmem_limit_bytes=8 * 2**20),
-        name="field",
-    )(*args)
+        name="own",
+    )(field, lengthscale[None])
 
 
 def swapped(value):
@@ -251,10 +271,12 @@
 def on_device(coords, alpha, probe_solves, probes, lengthscale):
     half_inv = 1.0 / (2.0 * probes.shape[0])
     hops = lax.axis_size("blk") // 8
-    field, *own = make_field(coords, alpha, probe_solves, probes, lengthscale)
+    field = make_field(coords, alpha, probe_solves, probes)
     mate = swapped(field)
     near = toward(field, -2, 2)
-    acc, *own_mate = visit(half_inv, ((0, 0),), [mate], [own], [], n_form=1)
+    scale, *own = make_own(field, lengthscale)
+    mate, own = lax.optimization_barrier((mate, own))
+    acc, *own_mate = visit(half_inv, scale, ((0, 0),), [mate], [own], [], n_form=1)
     later, acc = lax.optimization_barrier((field, acc))
     cross = toward(later, 3, -3)
     near, acc = lax.optimization_barrier((near, acc))
@@ -262,15 +284,15 @@
     for hop in range(1, hops):
         here, there = near, cross
         near = toward(here, -2, 2)
-        accs = visit(half_inv, ((0, 1), (0, 0)), [here], [own, own_mate], accs)
+        accs = visit(half_inv, scale, ((0, 1), (0, 0)), [here], [own, own_mate], accs)
         there, near_accs = lax.optimization_barrier((there, accs))
         cross = toward(there, -2, 2)
-        accs = visit(half_inv, ((0, 1), (0, 0)), [there], [own, own_mate], near_accs)
-    (acc,) = visit(half_inv, ((0, 0),), [near], [own_mate], accs[1:])
+        accs = visit(half_inv, scale, ((0, 1), (0, 0)), [there], [own, own_mate], near_accs)
+    (acc,) = visit(half_inv, scale, ((0, 0),), [near], [own_mate], accs[1:])
     cross, acc = lax.optimization_barrier((cross, acc))
-    _, theirs = visit(half_inv, ((0, 0),), [cross], [own_mate], [acc], done=(0,), fields=[mate])
+    _, theirs = visit(half_inv, scale, ((0, 0),), [cross], [own_mate], [acc], done=(0,), fields=[mate])
     theirs = swapped(theirs)
-    _, mine = visit(half_inv, ((0, 0),), [near], [own], accs[:1], done=(0,), fields=[field])
+    _, mine = visit(half_inv, scale, ((0, 0),), [near], [own], accs[:1], done=(0,), fields=[field])
     total = mine + theirs
     return (-(root_five / 3.0) / lengthscale)[:, None] * total
 

time: 50.5 us -> 49.8 us (0.986)
  waiting for transfers between devices: 3.84 us -> 3.1 us
  local copies, waits for them, and re-layouts: 0.63 us -> 0.02 us
    ppermute x8, starting transfers between devices: 6.23 us -> 6.96 us  [toward(): return lax.ppermute(value, 'blk', pairs)]
    unnamed x8, local copies, waits for them, and re-layouts: 0.63 us -> 0.02 us
    ppermute x8, waiting for transfers between devices: 2.77 us -> 2.17 us  [toward(): return lax.ppermute(value, 'blk', pairs)]
  transfers between devices with their start and end apart: 10 -> 10, of which waited for: 7 -> 6; matrix products, arithmetic and copies ran while one was open for 0% -> 0% of each run, Pallas kernels for 39% -> 40%
where the time goes in v2:
time: 49.8 us; the launch traced here: 49.7 us
  starting transfers between devices  23.2 us (47%)
  Pallas kernels  21.5 us (43%)
  waiting for transfers between devices  3.1 us (6%)
  other arithmetic  1.64 us (3%)
    pallas_call x10, Pallas kernels, visit(): pl.pallas_call(functools.partial(visit_kernel, half_inv, pairs, len(vis),...  21.4 us
    ppermute x2, starting transfers between devices, swapped(): lax.ppermute(value, 'blk', [(b, b + 1 - 2 * (b % 2)) for b in range(count)])  16.3 us
    ppermute x8, starting transfers between devices, toward(): return lax.ppermute(value, 'blk', pairs)  6.96 us
    ppermute x8, waiting for transfers between devices, toward(): return lax.ppermute(value, 'blk', pairs)  2.17 us
  transfers between devices with their start and end apart: 10, of which 6 were waited for; matrix products, arithmetic and copies ran while one was open for 0% of the time, Pallas kernels for 40%

profile of v2, /device:TPU:69, one launch (start us, length us, event | category | flops | bytes accessed | tf_op | source)
XLA Modules:
  0.0 49.7 jit_solution(15135598282223708880)
XLA Ops:
  0.0 0.9 %broadcast_multiply_fusion.coords = f32[32,768]{1,0:T(8,128)S(1)} fusion(f32[32,768]{1,0:T(8,128)} %param.5), kind=kLoop, calls=%fused_computation.1 | loop fusion | flops 24576 | bytes 196608 | tf_op jit(solution)/shard_map/mul | solution.py:222
  1.0 10.0 %collective-permute-start.1 = (f32[64,768]{1,0:T(8,128)S(1)}, f32[64,768]{1,0:T(8,128)S(1)}, u32[]{:S(2)}, u32[]{:S(2)}) collective-permute-start(f32[64,768]{1,0:T(8,128)S(1)} %field.1.refs_5_), channel_id=1, source_target_pairs={{0,1},{1,0},{2,3},{3,2},{4,5},{5,4},{6,7},{7,6},{8,9},{9,8},{10,11... | collective-permute-start | bytes 589832 | tf_op jit(solution)/shard_map/ppermute | solution.py:262
  11.2 0.9 %collective-permute-done.1.refs_1_.refs_5_ = f32[64,768]{1,0:T(8,128)S(1)} collective-permute-done((f32[64,768]{1,0:T(8,128)S(1)}, f32[64,768]{1,0:T(8,128)S(1)}, u32[]{:S(2)}, u32[]{:S(2)}) %collective-permute-start.1) | collective-permute-done | bytes 196640 | tf_op jit(solution)/shard_map/ppermute | solution.py:262
  12.1 1.5 %visit.10 = (f32[80,768]{1,0:T(8,128)S(1)}, bf16[144,768]{1,0:T(8,128)(2,1)S(1)}, bf16[128,768]{1,0:T(8,128)(2,1)S(1)}) custom-call(f32[32,128]{1,0:T(8,128)S(1)} %get-tuple-element.43.refs_0_, f32[64,768]{1,0:T(8,128)S(1)} %collective-permute-done.1.refs_1_.refs_5_, bf16[144,768]{1,0:T(8,128)(2,1)S(1)} %get-tuple-element.47.refs_2_, ...), custom_call_target="tpu_custom_call" | custom-call | flops 1000000000 | bytes 1000000 | tf_op jit(solution)/shard_map/visit/pallas_call | solution.py:192
  13.6 4.2 %collective-permute-start.5 = (f32[64,768]{1,0:T(8,128)S(1)}, f32[64,768]{1,0:T(8,128)S(1)}, u32[]{:S(2)}, u32[]{:S(2)}) collective-permute-start(f32[64,768]{1,0:T(8,128)S(1)} %field.1.refs_5_), channel_id=1, source_target_pairs={{0,3},{1,30},{2,5},{3,0},{4,7},{5,2},{6,9},{7,4},{8,11},{9,6},{10,... | collective-permute-start | bytes 589832 | tf_op jit(solution)/shard_map/ppermute | solution.py:268
  17.8 0.4 collective-permute-start.2
  18.3 2.5 %visit.11 = (f32[80,768]{1,0:T(8,128)S(1)}, f32[80,768]{1,0:T(8,128)S(1)}) custom-call(f32[32,128]{1,0:T(8,128)S(1)} %get-tuple-element.43.refs_0_, f32[64,768]{1,0:T(8,128)S(1)} %collective-permute-done.refs_1_, bf16[144,768]{1,0:T(8,128)(2,1)S(1)} %get-tuple-element.47.refs_2_, ...), custom_call_target="tpu_custom_call", output_to_operand_aliasing={{0}: (6, {})} | custom-call | flops 2000000000 | bytes 1000000 | tf_op jit(solution)/shard_map/visit/pallas_call | solution.py:192
  20.8 0.2 collective-permute-done.5.refs_1_
  21.1 1.5 %collective-permute-start.6 = (f32[64,768]{1,0:T(8,128)S(1)}, f32[64,768]{1,0:T(8,128)S(1)}, u32[]{:S(2)}, u32[]{:S(2)}) collective-permute-start(f32[64,768]{1,0:T(8,128)S(1)} %collective-permute-done.5.refs_1_), channel_id=1, source_target_pairs={{0,30},{1,3},{2,0},{3,5},{4,2},{5,7},{6,4},{7,9},{8,6},{9,11},{10,... | collective-permute-start | bytes 589832 | tf_op jit(solution)/shard_map/ppermute | solution.py:268
  22.6 2.6 %visit.12 = (f32[80,768]{1,0:T(8,128)S(1)}, f32[80,768]{1,0:T(8,128)S(1)}) custom-call(f32[32,128]{1,0:T(8,128)S(1)} %get-tuple-element.43.refs_0_, f32[64,768]{1,0:T(8,128)S(1)} %collective-permute-done.5.refs_1_, bf16[144,768]{1,0:T(8,128)(2,1)S(1)} %get-tuple-element.47.refs_2_, ...), custom_call_target="tpu_custom_call", output_to_operand_aliasing={{0}: (6, {}), {1}: (7, {})} | custom-call | flops 2000000000 | bytes 1000000 | tf_op jit(solution)/shard_map/visit/pallas_call | solution.py:192
  25.3 2.6 %visit.13 = (f32[80,768]{1,0:T(8,128)S(1)}, f32[80,768]{1,0:T(8,128)S(1)}) custom-call(f32[32,128]{1,0:T(8,128)S(1)} %get-tuple-element.43.refs_0_, f32[64,768]{1,0:T(8,128)S(1)} %collective-permute-done.2.refs_1_, bf16[144,768]{1,0:T(8,128)(2,1)S(1)} %get-tuple-element.47.refs_2_, ...), custom_call_target="tpu_custom_call", output_to_operand_aliasing={{0}: (6, {}), {1}: (7, {})} | custom-call | flops 2000000000 | bytes 1000000 | tf_op jit(solution)/shard_map/visit/pallas_call | solution.py:192
  27.9 0.3 collective-permute-start.7
  28.2 2.6 %visit.14 = (f32[80,768]{1,0:T(8,128)S(1)}, f32[80,768]{1,0:T(8,128)S(1)}) custom-call(f32[32,128]{1,0:T(8,128)S(1)} %get-tuple-element.43.refs_0_, f32[64,768]{1,0:T(8,128)S(1)} %collective-permute-done.6.refs_1_, bf16[144,768]{1,0:T(8,128)(2,1)S(1)} %get-tuple-element.47.refs_2_, ...), custom_call_target="tpu_custom_call", output_to_operand_aliasing={{0}: (6, {}), {1}: (7, {})} | custom-call | flops 2000000000 | bytes 1000000 | tf_op jit(solution)/shard_map/visit/pallas_call | solution.py:192
  30.8 0.2 collective-permute-done.3.refs_1_
  31.0 2.6 %visit.15 = (f32[80,768]{1,0:T(8,128)S(1)}, f32[80,768]{1,0:T(8,128)S(1)}) custom-call(f32[32,128]{1,0:T(8,128)S(1)} %get-tuple-element.43.refs_0_, f32[64,768]{1,0:T(8,128)S(1)} %collective-permute-done.3.refs_1_, bf16[144,768]{1,0:T(8,128)(2,1)S(1)} %get-tuple-element.47.refs_2_, ...), custom_call_target="tpu_custom_call", output_to_operand_aliasing={{0}: (6, {}), {1}: (7, {})} | custom-call | flops 2000000000 | bytes 1000000 | tf_op jit(solution)/shard_map/visit/pallas_call | solution.py:192
  33.6 0.3 collective-permute-done.7.refs_1_
  34.0 0.4 collective-permute-start.8
  34.3 2.6 %visit.16 = (f32[80,768]{1,0:T(8,128)S(1)}, f32[80,768]{1,0:T(8,128)S(1)}) custom-call(f32[32,128]{1,0:T(8,128)S(1)} %get-tuple-element.43.refs_0_, f32[64,768]{1,0:T(8,128)S(1)} %collective-permute-done.7.refs_1_, bf16[144,768]{1,0:T(8,128)(2,1)S(1)} %get-tuple-element.47.refs_2_, ...), custom_call_target="tpu_custom_call", output_to_operand_aliasing={{0}: (6, {}), {1}: (7, {})} | custom-call | flops 2000000000 | bytes 1000000 | tf_op jit(solution)/shard_map/visit/pallas_call | solution.py:192
  36.9 1.5 %visit.18.refs_4_ = f32[80,768]{1,0:T(8,128)S(1)} custom-call(f32[32,128]{1,0:T(8,128)S(1)} %get-tuple-element.43.refs_0_, f32[64,768]{1,0:T(8,128)S(1)} %collective-permute-done.4.refs_1_, bf16[144,768]{1,0:T(8,128)(2,1)S(1)} %get-tuple-element.53.refs_4_.refs_2_, ...), custom_call_target="tpu_custom_call", output_to_operand_aliasing={{}: (4, {})} | custom-call | flops 1000000000 | bytes 1000000 | tf_op jit(solution)/shard_map/visit/pallas_call | solution.py:192
  38.4 1.3 %collective-permute-done.8.refs_1_ = f32[64,768]{1,0:T(8,128)S(1)} collective-permute-done((f32[64,768]{1,0:T(8,128)S(1)}, f32[64,768]{1,0:T(8,128)S(1)}, u32[]{:S(2)}, u32[]{:S(2)}) %collective-permute-start.8) | collective-permute-done | bytes 196640 | tf_op jit(solution)/shard_map/ppermute | solution.py:268
  39.7 1.5 %visit.19 = (f32[80,768]{1,0:T(8,128)S(1)}, f32[32,768]{1,0:T(8,128)S(1)}) custom-call(f32[32,128]{1,0:T(8,128)S(1)} %get-tuple-element.43.refs_0_, f32[64,768]{1,0:T(8,128)S(1)} %collective-permute-done.8.refs_1_, bf16[144,768]{1,0:T(8,128)(2,1)S(1)} %get-tuple-element.53.refs_4_.refs_2_, ...), custom_call_target="tpu_custom_call", output_to_operand_aliasing={{0}: (4, {})} | custom-call | flops 1000000000 | bytes 1000000 | tf_op jit(solution)/shard_map/visit/pallas_call | solution.py:192
  41.2 6.3 %collective-permute-start.9 = (f32[32,768]{1,0:T(8,128)S(1)}, f32[32,768]{1,0:T(8,128)S(1)}, u32[]{:S(2)}, u32[]{:S(2)}) collective-permute-start(f32[32,768]{1,0:T(8,128)S(1)} %get-tuple-element.80), channel_id=1, source_target_pairs={{0,1},{1,0},{2,3},{3,2},{4,5},{5,4},{6,7},{7,6},{8,9},{9,8},{10,11... | collective-permute-start | bytes 294920 | tf_op jit(solution)/shard_map/ppermute | solution.py:262
  47.5 1.5 %visit.17 = (f32[80,768]{1,0:T(8,128)S(1)}, f32[32,768]{1,0:T(8,128)S(1)}) custom-call(f32[32,128]{1,0:T(8,128)S(1)} %get-tuple-element.43.refs_0_, f32[64,768]{1,0:T(8,128)S(1)} %collective-permute-done.4.refs_1_, bf16[144,768]{1,0:T(8,128)(2,1)S(1)} %get-tuple-element.47.refs_2_, ...), custom_call_target="tpu_custom_call", output_to_operand_aliasing={{0}: (4, {})} | custom-call | flops 1000000000 | bytes 1000000 | tf_op jit(solution)/shard_map/visit/pallas_call | solution.py:192
  49.0 0.7 %add_multiply_fusion = f32[32,768]{1,0:T(8,128)} fusion(f32[32,768]{1,0:T(8,128)S(1)} %get-tuple-element.76, f32[32,768]{1,0:T(8,128)S(1)} %collective-permute-done.9, f32[32]{0:T(128)S(1)} %broadcast_divide_fusion), kind=kLoop, calls=%fused_computation | loop fusion | flops 49152 | bytes 295040 | tf_op jit(solution)/shard_map/mul | solution.py:297
  (19 shorter events, 0.5 us)
Async XLA Ops:
  0.0 0.9 %copy-start = (f32[15,768]{1,0:T(8,128)S(1)}, f32[15,768]{1,0:T(8,128)}, u32[]{:S(2)}) copy-start(f32[15,768]{1,0:T(8,128)} %solves.1) | copy-start | bytes 138244
  0.0 0.9 %copy-start.1 = (f32[15,768]{1,0:T(8,128)S(1)}, f32[15,768]{1,0:T(8,128)}, u32[]{:S(2)}) copy-start(f32[15,768]{1,0:T(8,128)} %probes.1) | copy-start | bytes 138244
  0.0 0.9 %copy-start.2 = (f32[768]{0:T(1024)S(1)}, f32[768]{0:T(1024)}, u32[]{:S(2)}) copy-start(f32[768]{0:T(1024)} %param.6) | copy-start | bytes 9220
  1.0 10.0 %copy-start.3 = (f32[32]{0:T(128)S(1)}, f32[32]{0:T(128)}, u32[]{:S(2)}) copy-start(f32[32]{0:T(128)} %param.9) | copy-start | bytes 388
  1.0 11.1 %collective-permute-start.1 = (f32[64,768]{1,0:T(8,128)S(1)}, f32[64,768]{1,0:T(8,128)S(1)}, u32[]{:S(2)}, u32[]{:S(2)}) collective-permute-start(f32[64,768]{1,0:T(8,128)S(1)} %field.1.refs_5_), channel_id=1, source_target_pairs={{0,1},{1,0},{2,3},{3,2},{4,5},{5,4},{6,7},{7,6},{8,9},{9,8},{10,11... | collective-permute-start | bytes 589832 | tf_op jit(solution)/shard_map/ppermute | solution.py:262
  11.0 6.8 %collective-permute-start = (f32[64,768]{1,0:T(8,128)S(1)}, f32[64,768]{1,0:T(8,128)S(1)}, u32[]{:S(2)}, u32[]{:S(2)}) collective-permute-start(f32[64,768]{1,0:T(8,128)S(1)} %field.1.refs_5_), channel_id=1, source_target_pairs={{0,30},{1,3},{2,0},{3,5},{4,2},{5,7},{6,4},{7,9},{8,6},{9,11},{10,... | collective-permute-start | bytes 589832 | tf_op jit(solution)/shard_map/ppermute | solution.py:268
  13.6 7.5 %collective-permute-start.5 = (f32[64,768]{1,0:T(8,128)S(1)}, f32[64,768]{1,0:T(8,128)S(1)}, u32[]{:S(2)}, u32[]{:S(2)}) collective-permute-start(f32[64,768]{1,0:T(8,128)S(1)} %field.1.refs_5_), channel_id=1, source_target_pairs={{0,3},{1,30},{2,5},{3,0},{4,7},{5,2},{6,9},{7,4},{8,11},{9,6},{10,... | collective-permute-start | bytes 589832 | tf_op jit(solution)/shard_map/ppermute | solution.py:268
  17.8 7.4 %collective-permute-start.2 = (f32[64,768]{1,0:T(8,128)S(1)}, f32[64,768]{1,0:T(8,128)S(1)}, u32[]{:S(2)}, u32[]{:S(2)}) collective-permute-start(f32[64,768]{1,0:T(8,128)S(1)} %collective-permute-done.refs_1_), channel_id=1, source_target_pairs={{0,30},{1,3},{2,0},{3,5},{4,2},{5,7},{6,4},{7,9},{8,6},{9,11},{10,... | collective-permute-start | bytes 589832 | tf_op jit(solution)/shard_map/ppermute | solution.py:268
  21.1 6.9 %collective-permute-start.6 = (f32[64,768]{1,0:T(8,128)S(1)}, f32[64,768]{1,0:T(8,128)S(1)}, u32[]{:S(2)}, u32[]{:S(2)}) collective-permute-start(f32[64,768]{1,0:T(8,128)S(1)} %collective-permute-done.5.refs_1_), channel_id=1, source_target_pairs={{0,30},{1,3},{2,0},{3,5},{4,2},{5,7},{6,4},{7,9},{8,6},{9,11},{10,... | collective-permute-start | bytes 589832 | tf_op jit(solution)/shard_map/ppermute | solution.py:268
  25.2 5.8 %collective-permute-start.3 = (f32[64,768]{1,0:T(8,128)S(1)}, f32[64,768]{1,0:T(8,128)S(1)}, u32[]{:S(2)}, u32[]{:S(2)}) collective-permute-start(f32[64,768]{1,0:T(8,128)S(1)} %collective-permute-done.2.refs_1_), channel_id=1, source_target_pairs={{0,30},{1,3},{2,0},{3,5},{4,2},{5,7},{6,4},{7,9},{8,6},{9,11},{10,... | collective-permute-start | bytes 589832 | tf_op jit(solution)/shard_map/ppermute | solution.py:268
  27.9 6.0 %collective-permute-start.7 = (f32[64,768]{1,0:T(8,128)S(1)}, f32[64,768]{1,0:T(8,128)S(1)}, u32[]{:S(2)}, u32[]{:S(2)}) collective-permute-start(f32[64,768]{1,0:T(8,128)S(1)} %collective-permute-done.6.refs_1_), channel_id=1, source_target_pairs={{0,30},{1,3},{2,0},{3,5},{4,2},{5,7},{6,4},{7,9},{8,6},{9,11},{10,... | collective-permute-start | bytes 589832 | tf_op jit(solution)/shard_map/ppermute | solution.py:268
  31.0 5.9 %collective-permute-start.4 = (f32[64,768]{1,0:T(8,128)S(1)}, f32[64,768]{1,0:T(8,128)S(1)}, u32[]{:S(2)}, u32[]{:S(2)}) collective-permute-start(f32[64,768]{1,0:T(8,128)S(1)} %collective-permute-done.3.refs_1_), channel_id=1, source_target_pairs={{0,30},{1,3},{2,0},{3,5},{4,2},{5,7},{6,4},{7,9},{8,6},{9,11},{10,... | collective-permute-start | bytes 589832 | tf_op jit(solution)/shard_map/ppermute | solution.py:268
  34.0 5.7 %collective-permute-start.8 = (f32[64,768]{1,0:T(8,128)S(1)}, f32[64,768]{1,0:T(8,128)S(1)}, u32[]{:S(2)}, u32[]{:S(2)}) collective-permute-start(f32[64,768]{1,0:T(8,128)S(1)} %collective-permute-done.7.refs_1_), channel_id=1, source_target_pairs={{0,30},{1,3},{2,0},{3,5},{4,2},{5,7},{6,4},{7,9},{8,6},{9,11},{10,... | collective-permute-start | bytes 589832 | tf_op jit(solution)/shard_map/ppermute | solution.py:268
  41.2 7.8 %collective-permute-start.9 = (f32[32,768]{1,0:T(8,128)S(1)}, f32[32,768]{1,0:T(8,128)S(1)}, u32[]{:S(2)}, u32[]{:S(2)}) collective-permute-start(f32[32,768]{1,0:T(8,128)S(1)} %get-tuple-element.80), channel_id=1, source_target_pairs={{0,1},{1,0},{2,3},{3,2},{4,5},{5,4},{6,7},{7,6},{8,9},{9,8},{10,11... | collective-permute-start | bytes 294920 | tf_op jit(solution)/shard_map/ppermute | solution.py:262

commit v3 on v2

--- a/solution.py
+++ b/solution.py
@@ -37,7 +37,7 @@
 
 def scaled_halves(field, scale):
     wide = jnp.concatenate([scale] * (field.shape[1] // scale.shape[1]), 1)
-    high, low = halves(field[:DIM] * wide)
+    high, low = halves((field[:DIM] - wide[DIM:]) * wide[:DIM])
     return high, low, high.astype(f32) + low.astype(f32)
 
 
@@ -236,7 +236,10 @@
     row = lax.broadcasted_iota(jnp.int32, (size, size), 0)
     col = lax.broadcasted_iota(jnp.int32, (size, size), 1)
     column = jnp.sum(jnp.where(row == col, spread, 0.0), 1, keepdims=True)
-    scale = jnp.broadcast_to(1.0 / column, scale_ref.shape)
+    centre = jnp.mean(field[:DIM, :], 1, keepdims=True)
+    scale = jnp.concatenate(
+        [jnp.broadcast_to(part, (DIM, scale_ref.shape[1])) for part in (1.0 / column, centre)], 0
+    )
     scale_ref[...] = scale
     own_forms(field[...], scale, dist_ref, coup_ref)
 
@@ -246,7 +249,7 @@
     return pl.pallas_call(
         scale_kernel,
         out_shape=[
-            jax.ShapeDtypeStruct((DIM, 128), f32),
+            jax.ShapeDtypeStruct((2 * DIM, 128), f32),
             jax.ShapeDtypeStruct((4 * DIM + GROUP, points), bf16),
             jax.ShapeDtypeStruct((8 * GROUP, points), bf16),
         ],

time: 49.8 us -> 49.9 us (level)
  no operation moved by 1% of the time
where the time goes in v3:
time: 49.9 us; the launch traced here: 49.7 us
  starting transfers between devices  23.3 us (47%)
  Pallas kernels  21.6 us (43%)
  waiting for transfers between devices  3.03 us (6%)
  other arithmetic  1.64 us (3%)
    pallas_call x10, Pallas kernels, visit(): pl.pallas_call(functools.partial(visit_kernel, half_inv, pairs, len(vis),...  21.4 us
    ppermute x2, starting transfers between devices, swapped(): lax.ppermute(value, 'blk', [(b, b + 1 - 2 * (b % 2)) for b in range(count)])  16.2 us
    ppermute x8, starting transfers between devices, toward(): return lax.ppermute(value, 'blk', pairs)  7.03 us
    ppermute x8, waiting for transfers between devices, toward(): return lax.ppermute(value, 'blk', pairs)  2.11 us
  transfers between devices with their start and end apart: 10, of which 6 were waited for; matrix products, arithmetic and copies ran while one was open for 0% of the time, Pallas kernels for 40%

profile of v3, /device:TPU:69, one launch (start us, length us, event | category | flops | bytes accessed | tf_op | source)
XLA Modules:
  0.0 49.7 jit_solution(11244772773305631651)
XLA Ops:
  0.0 0.9 %broadcast_multiply_fusion.coords = f32[32,768]{1,0:T(8,128)S(1)} fusion(f32[32,768]{1,0:T(8,128)} %param.5), kind=kLoop, calls=%fused_computation.1 | loop fusion | flops 24576 | bytes 196608 | tf_op jit(solution)/shard_map/mul | solution.py:222
  1.0 10.0 %collective-permute-start.1 = (f32[64,768]{1,0:T(8,128)S(1)}, f32[64,768]{1,0:T(8,128)S(1)}, u32[]{:S(2)}, u32[]{:S(2)}) collective-permute-start(f32[64,768]{1,0:T(8,128)S(1)} %field.1.refs_5_), channel_id=1, source_target_pairs={{0,1},{1,0},{2,3},{3,2},{4,5},{5,4},{6,7},{7,6},{8,9},{9,8},{10,11... | collective-permute-start | bytes 589832 | tf_op jit(solution)/shard_map/ppermute | solution.py:265
  11.2 0.9 %collective-permute-done.1.refs_1_.refs_5_ = f32[64,768]{1,0:T(8,128)S(1)} collective-permute-done((f32[64,768]{1,0:T(8,128)S(1)}, f32[64,768]{1,0:T(8,128)S(1)}, u32[]{:S(2)}, u32[]{:S(2)}) %collective-permute-start.1) | collective-permute-done | bytes 196640 | tf_op jit(solution)/shard_map/ppermute | solution.py:265
  12.1 1.5 %visit.10 = (f32[80,768]{1,0:T(8,128)S(1)}, bf16[144,768]{1,0:T(8,128)(2,1)S(1)}, bf16[128,768]{1,0:T(8,128)(2,1)S(1)}) custom-call(f32[64,128]{1,0:T(8,128)S(1)} %get-tuple-element.43.refs_0_, f32[64,768]{1,0:T(8,128)S(1)} %collective-permute-done.1.refs_1_.refs_5_, bf16[144,768]{1,0:T(8,128)(2,1)S(1)} %get-tuple-element.47.refs_2_, ...), custom_call_target="tpu_custom_call" | custom-call | flops 1000000000 | bytes 1000000 | tf_op jit(solution)/shard_map/visit/pallas_call | solution.py:192
  13.6 4.1 %collective-permute-start.5 = (f32[64,768]{1,0:T(8,128)S(1)}, f32[64,768]{1,0:T(8,128)S(1)}, u32[]{:S(2)}, u32[]{:S(2)}) collective-permute-start(f32[64,768]{1,0:T(8,128)S(1)} %field.1.refs_5_), channel_id=1, source_target_pairs={{0,3},{1,30},{2,5},{3,0},{4,7},{5,2},{6,9},{7,4},{8,11},{9,6},{10,... | collective-permute-start | bytes 589832 | tf_op jit(solution)/shard_map/ppermute | solution.py:271
  17.8 0.5 collective-permute-start.2
  18.3 2.5 %visit.11 = (f32[80,768]{1,0:T(8,128)S(1)}, f32[80,768]{1,0:T(8,128)S(1)}) custom-call(f32[64,128]{1,0:T(8,128)S(1)} %get-tuple-element.43.refs_0_, f32[64,768]{1,0:T(8,128)S(1)} %collective-permute-done.refs_1_, bf16[144,768]{1,0:T(8,128)(2,1)S(1)} %get-tuple-element.47.refs_2_, ...), custom_call_target="tpu_custom_call", output_to_operand_aliasing={{0}: (6, {})} | custom-call | flops 2000000000 | bytes 1000000 | tf_op jit(solution)/shard_map/visit/pallas_call | solution.py:192
  20.9 0.2 collective-permute-done.5.refs_1_
  21.1 1.6 %collective-permute-start.6 = (f32[64,768]{1,0:T(8,128)S(1)}, f32[64,768]{1,0:T(8,128)S(1)}, u32[]{:S(2)}, u32[]{:S(2)}) collective-permute-start(f32[64,768]{1,0:T(8,128)S(1)} %collective-permute-done.5.refs_1_), channel_id=1, source_target_pairs={{0,30},{1,3},{2,0},{3,5},{4,2},{5,7},{6,4},{7,9},{8,6},{9,11},{10,... | collective-permute-start | bytes 589832 | tf_op jit(solution)/shard_map/ppermute | solution.py:271
  22.6 2.6 %visit.12 = (f32[80,768]{1,0:T(8,128)S(1)}, f32[80,768]{1,0:T(8,128)S(1)}) custom-call(f32[64,128]{1,0:T(8,128)S(1)} %get-tuple-element.43.refs_0_, f32[64,768]{1,0:T(8,128)S(1)} %collective-permute-done.5.refs_1_, bf16[144,768]{1,0:T(8,128)(2,1)S(1)} %get-tuple-element.47.refs_2_, ...), custom_call_target="tpu_custom_call", output_to_operand_aliasing={{0}: (6, {}), {1}: (7, {})} | custom-call | flops 2000000000 | bytes 1000000 | tf_op jit(solution)/shard_map/visit/pallas_call | solution.py:192
  25.4 2.6 %visit.13 = (f32[80,768]{1,0:T(8,128)S(1)}, f32[80,768]{1,0:T(8,128)S(1)}) custom-call(f32[64,128]{1,0:T(8,128)S(1)} %get-tuple-element.43.refs_0_, f32[64,768]{1,0:T(8,128)S(1)} %collective-permute-done.2.refs_1_, bf16[144,768]{1,0:T(8,128)(2,1)S(1)} %get-tuple-element.47.refs_2_, ...), custom_call_target="tpu_custom_call", output_to_operand_aliasing={{0}: (6, {}), {1}: (7, {})} | custom-call | flops 2000000000 | bytes 1000000 | tf_op jit(solution)/shard_map/visit/pallas_call | solution.py:192
  28.0 0.3 collective-permute-start.7
  28.3 2.6 %visit.14 = (f32[80,768]{1,0:T(8,128)S(1)}, f32[80,768]{1,0:T(8,128)S(1)}) custom-call(f32[64,128]{1,0:T(8,128)S(1)} %get-tuple-element.43.refs_0_, f32[64,768]{1,0:T(8,128)S(1)} %collective-permute-done.6.refs_1_, bf16[144,768]{1,0:T(8,128)(2,1)S(1)} %get-tuple-element.47.refs_2_, ...), custom_call_target="tpu_custom_call", output_to_operand_aliasing={{0}: (6, {}), {1}: (7, {})} | custom-call | flops 2000000000 | bytes 1000000 | tf_op jit(solution)/shard_map/visit/pallas_call | solution.py:192
  30.9 0.2 collective-permute-done.3.refs_1_
  31.1 2.6 %visit.15 = (f32[80,768]{1,0:T(8,128)S(1)}, f32[80,768]{1,0:T(8,128)S(1)}) custom-call(f32[64,128]{1,0:T(8,128)S(1)} %get-tuple-element.43.refs_0_, f32[64,768]{1,0:T(8,128)S(1)} %collective-permute-done.3.refs_1_, bf16[144,768]{1,0:T(8,128)(2,1)S(1)} %get-tuple-element.47.refs_2_, ...), custom_call_target="tpu_custom_call", output_to_operand_aliasing={{0}: (6, {}), {1}: (7, {})} | custom-call | flops 2000000000 | bytes 1000000 | tf_op jit(solution)/shard_map/visit/pallas_call | solution.py:192
  33.7 0.3 collective-permute-done.7.refs_1_
  34.0 0.4 collective-permute-start.8
  34.4 2.6 %visit.16 = (f32[80,768]{1,0:T(8,128)S(1)}, f32[80,768]{1,0:T(8,128)S(1)}) custom-call(f32[64,128]{1,0:T(8,128)S(1)} %get-tuple-element.43.refs_0_, f32[64,768]{1,0:T(8,128)S(1)} %collective-permute-done.7.refs_1_, bf16[144,768]{1,0:T(8,128)(2,1)S(1)} %get-tuple-element.47.refs_2_, ...), custom_call_target="tpu_custom_call", output_to_operand_aliasing={{0}: (6, {}), {1}: (7, {})} | custom-call | flops 2000000000 | bytes 1000000 | tf_op jit(solution)/shard_map/visit/pallas_call | solution.py:192
  37.0 1.5 %visit.18.refs_4_ = f32[80,768]{1,0:T(8,128)S(1)} custom-call(f32[64,128]{1,0:T(8,128)S(1)} %get-tuple-element.43.refs_0_, f32[64,768]{1,0:T(8,128)S(1)} %collective-permute-done.4.refs_1_, bf16[144,768]{1,0:T(8,128)(2,1)S(1)} %get-tuple-element.53.refs_4_.refs_2_, ...), custom_call_target="tpu_custom_call", output_to_operand_aliasing={{}: (4, {})} | custom-call | flops 1000000000 | bytes 1000000 | tf_op jit(solution)/shard_map/visit/pallas_call | solution.py:192
  38.5 1.2 %collective-permute-done.8.refs_1_ = f32[64,768]{1,0:T(8,128)S(1)} collective-permute-done((f32[64,768]{1,0:T(8,128)S(1)}, f32[64,768]{1,0:T(8,128)S(1)}, u32[]{:S(2)}, u32[]{:S(2)}) %collective-permute-start.8) | collective-permute-done | bytes 196640 | tf_op jit(solution)/shard_map/ppermute | solution.py:271
  39.7 1.5 %visit.19 = (f32[80,768]{1,0:T(8,128)S(1)}, f32[32,768]{1,0:T(8,128)S(1)}) custom-call(f32[64,128]{1,0:T(8,128)S(1)} %get-tuple-element.43.refs_0_, f32[64,768]{1,0:T(8,128)S(1)} %collective-permute-done.8.refs_1_, bf16[144,768]{1,0:T(8,128)(2,1)S(1)} %get-tuple-element.53.refs_4_.refs_2_, ...), custom_call_target="tpu_custom_call", output_to_operand_aliasing={{0}: (4, {})} | custom-call | flops 1000000000 | bytes 1000000 | tf_op jit(solution)/shard_map/visit/pallas_call | solution.py:192
  41.2 6.2 %collective-permute-start.9 = (f32[32,768]{1,0:T(8,128)S(1)}, f32[32,768]{1,0:T(8,128)S(1)}, u32[]{:S(2)}, u32[]{:S(2)}) collective-permute-start(f32[32,768]{1,0:T(8,128)S(1)} %get-tuple-element.80), channel_id=1, source_target_pairs={{0,1},{1,0},{2,3},{3,2},{4,5},{5,4},{6,7},{7,6},{8,9},{9,8},{10,11... | collective-permute-start | bytes 294920 | tf_op jit(solution)/shard_map/ppermute | solution.py:265
  47.5 1.5 %visit.17 = (f32[80,768]{1,0:T(8,128)S(1)}, f32[32,768]{1,0:T(8,128)S(1)}) custom-call(f32[64,128]{1,0:T(8,128)S(1)} %get-tuple-element.43.refs_0_, f32[64,768]{1,0:T(8,128)S(1)} %collective-permute-done.4.refs_1_, bf16[144,768]{1,0:T(8,128)(2,1)S(1)} %get-tuple-element.47.refs_2_, ...), custom_call_target="tpu_custom_call", output_to_operand_aliasing={{0}: (4, {})} | custom-call | flops 1000000000 | bytes 1000000 | tf_op jit(solution)/shard_map/visit/pallas_call | solution.py:192
  49.0 0.7 %add_multiply_fusion = f32[32,768]{1,0:T(8,128)} fusion(f32[32,768]{1,0:T(8,128)S(1)} %get-tuple-element.76, f32[32,768]{1,0:T(8,128)S(1)} %collective-permute-done.9, f32[32]{0:T(128)S(1)} %broadcast_divide_fusion), kind=kLoop, calls=%fused_computation | loop fusion | flops 49152 | bytes 295040 | tf_op jit(solution)/shard_map/mul | solution.py:300
  (19 shorter events, 0.5 us)
Async XLA Ops:
  0.0 0.9 %copy-start = (f32[15,768]{1,0:T(8,128)S(1)}, f32[15,768]{1,0:T(8,128)}, u32[]{:S(2)}) copy-start(f32[15,768]{1,0:T(8,128)} %solves.1) | copy-start | bytes 138244
  0.0 0.9 %copy-start.1 = (f32[15,768]{1,0:T(8,128)S(1)}, f32[15,768]{1,0:T(8,128)}, u32[]{:S(2)}) copy-start(f32[15,768]{1,0:T(8,128)} %probes.1) | copy-start | bytes 138244
  0.0 0.9 %copy-start.2 = (f32[768]{0:T(1024)S(1)}, f32[768]{0:T(1024)}, u32[]{:S(2)}) copy-start(f32[768]{0:T(1024)} %param.6) | copy-start | bytes 9220
  1.0 10.0 %copy-start.3 = (f32[32]{0:T(128)S(1)}, f32[32]{0:T(128)}, u32[]{:S(2)}) copy-start(f32[32]{0:T(128)} %param.9) | copy-start | bytes 388
  1.0 11.1 %collective-permute-start.1 = (f32[64,768]{1,0:T(8,128)S(1)}, f32[64,768]{1,0:T(8,128)S(1)}, u32[]{:S(2)}, u32[]{:S(2)}) collective-permute-start(f32[64,768]{1,0:T(8,128)S(1)} %field.1.refs_5_), channel_id=1, source_target_pairs={{0,1},{1,0},{2,3},{3,2},{4,5},{5,4},{6,7},{7,6},{8,9},{9,8},{10,11... | collective-permute-start | bytes 589832 | tf_op jit(solution)/shard_map/ppermute | solution.py:265
  11.0 6.8 %collective-permute-start = (f32[64,768]{1,0:T(8,128)S(1)}, f32[64,768]{1,0:T(8,128)S(1)}, u32[]{:S(2)}, u32[]{:S(2)}) collective-permute-start(f32[64,768]{1,0:T(8,128)S(1)} %field.1.refs_5_), channel_id=1, source_target_pairs={{0,30},{1,3},{2,0},{3,5},{4,2},{5,7},{6,4},{7,9},{8,6},{9,11},{10,... | collective-permute-start | bytes 589832 | tf_op jit(solution)/shard_map/ppermute | solution.py:271
  13.6 7.5 %collective-permute-start.5 = (f32[64,768]{1,0:T(8,128)S(1)}, f32[64,768]{1,0:T(8,128)S(1)}, u32[]{:S(2)}, u32[]{:S(2)}) collective-permute-start(f32[64,768]{1,0:T(8,128)S(1)} %field.1.refs_5_), channel_id=1, source_target_pairs={{0,3},{1,30},{2,5},{3,0},{4,7},{5,2},{6,9},{7,4},{8,11},{9,6},{10,... | collective-permute-start | bytes 589832 | tf_op jit(solution)/shard_map/ppermute | solution.py:271
  17.8 7.4 %collective-permute-start.2 = (f32[64,768]{1,0:T(8,128)S(1)}, f32[64,768]{1,0:T(8,128)S(1)}, u32[]{:S(2)}, u32[]{:S(2)}) collective-permute-start(f32[64,768]{1,0:T(8,128)S(1)} %collective-permute-done.refs_1_), channel_id=1, source_target_pairs={{0,30},{1,3},{2,0},{3,5},{4,2},{5,7},{6,4},{7,9},{8,6},{9,11},{10,... | collective-permute-start | bytes 589832 | tf_op jit(solution)/shard_map/ppermute | solution.py:271
  21.1 6.9 %collective-permute-start.6 = (f32[64,768]{1,0:T(8,128)S(1)}, f32[64,768]{1,0:T(8,128)S(1)}, u32[]{:S(2)}, u32[]{:S(2)}) collective-permute-start(f32[64,768]{1,0:T(8,128)S(1)} %collective-permute-done.5.refs_1_), channel_id=1, source_target_pairs={{0,30},{1,3},{2,0},{3,5},{4,2},{5,7},{6,4},{7,9},{8,6},{9,11},{10,... | collective-permute-start | bytes 589832 | tf_op jit(solution)/shard_map/ppermute | solution.py:271
  25.2 5.8 %collective-permute-start.3 = (f32[64,768]{1,0:T(8,128)S(1)}, f32[64,768]{1,0:T(8,128)S(1)}, u32[]{:S(2)}, u32[]{:S(2)}) collective-permute-start(f32[64,768]{1,0:T(8,128)S(1)} %collective-permute-done.2.refs_1_), channel_id=1, source_target_pairs={{0,30},{1,3},{2,0},{3,5},{4,2},{5,7},{6,4},{7,9},{8,6},{9,11},{10,... | collective-permute-start | bytes 589832 | tf_op jit(solution)/shard_map/ppermute | solution.py:271
  28.0 6.0 %collective-permute-start.7 = (f32[64,768]{1,0:T(8,128)S(1)}, f32[64,768]{1,0:T(8,128)S(1)}, u32[]{:S(2)}, u32[]{:S(2)}) collective-permute-start(f32[64,768]{1,0:T(8,128)S(1)} %collective-permute-done.6.refs_1_), channel_id=1, source_target_pairs={{0,30},{1,3},{2,0},{3,5},{4,2},{5,7},{6,4},{7,9},{8,6},{9,11},{10,... | collective-permute-start | bytes 589832 | tf_op jit(solution)/shard_map/ppermute | solution.py:271
  31.1 6.0 %collective-permute-start.4 = (f32[64,768]{1,0:T(8,128)S(1)}, f32[64,768]{1,0:T(8,128)S(1)}, u32[]{:S(2)}, u32[]{:S(2)}) collective-permute-start(f32[64,768]{1,0:T(8,128)S(1)} %collective-permute-done.3.refs_1_), channel_id=1, source_target_pairs={{0,30},{1,3},{2,0},{3,5},{4,2},{5,7},{6,4},{7,9},{8,6},{9,11},{10,... | collective-permute-start | bytes 589832 | tf_op jit(solution)/shard_map/ppermute | solution.py:271
  34.0 5.7 %collective-permute-start.8 = (f32[64,768]{1,0:T(8,128)S(1)}, f32[64,768]{1,0:T(8,128)S(1)}, u32[]{:S(2)}, u32[]{:S(2)}) collective-permute-start(f32[64,768]{1,0:T(8,128)S(1)} %collective-permute-done.7.refs_1_), channel_id=1, source_target_pairs={{0,30},{1,3},{2,0},{3,5},{4,2},{5,7},{6,4},{7,9},{8,6},{9,11},{10,... | collective-permute-start | bytes 589832 | tf_op jit(solution)/shard_map/ppermute | solution.py:271
  41.2 7.8 %collective-permute-start.9 = (f32[32,768]{1,0:T(8,128)S(1)}, f32[32,768]{1,0:T(8,128)S(1)}, u32[]{:S(2)}, u32[]{:S(2)}) collective-permute-start(f32[32,768]{1,0:T(8,128)S(1)} %get-tuple-element.80), channel_id=1, source_target_pairs={{0,1},{1,0},{2,3},{3,2},{4,5},{5,4},{6,7},{7,6},{8,9},{9,8},{10,11... | collective-permute-start | bytes 294920 | tf_op jit(solution)/shard_map/ppermute | solution.py:265

commit v4 on v3

--- a/solution.py
+++ b/solution.py
@@ -55,7 +55,9 @@
     points = field.shape[1]
     high, low, near = scaled_halves(field, scale)
     first, second = field[DIM : DIM + GROUP], field[DIM + GROUP :]
-    sums_ref[...] = jnp.concatenate([high, low, jnp.ones((GROUP, points), bf16)], 0)
+    sums = jnp.concatenate([high, low, jnp.ones((GROUP, points), bf16)], 0)
+    for index in range(points // BACK):
+        sums_ref[index] = sums[:, index * BACK : (index + 1) * BACK]
     square = jnp.broadcast_to(jnp.sum(near * near, 0, keepdims=True), first.shape)
     twice = [-2.0 * high, -2.0 * low]
     zero = jnp.zeros((256 - 4 * DIM - GROUP, points), bf16)
@@ -108,7 +110,7 @@
 
     def back(chunk, slot):
         v, o, start, begin = chunk
-        sums = sides[v][2][:, begin : begin + BACK]
+        sums = sides[v][2][begin // BACK]
         rows, cols = slice(begin, begin + BACK), slice(start, start + width)
         accs[o][:, cols] += dot(sums, high_ref[slot, rows, :]) + dot(sums, low_ref[slot, rows, :])
 
@@ -185,7 +187,7 @@
         scratch += [
             pltpu.VMEM((points, 256), bf16),
             pltpu.VMEM((points, 8 * GROUP), bf16),
-            pltpu.VMEM((SUMS, points), bf16),
+            pltpu.VMEM((points // BACK, SUMS, BACK), bf16),
         ]
     args = [scale, *vis, *[ref for forms in own for ref in forms], *accs, *fields]
     first = 1 + len(vis) + 2 * n_own

time: 49.9 us -> 49.8 us (level)
  no operation moved by 1% of the time
where the time goes in v4:
time: 49.8 us; the launch traced here: 49.7 us
  starting transfers between devices  23.2 us (47%)
  Pallas kernels  21.5 us (43%)
  waiting for transfers between devices  3.14 us (6%)
  other arithmetic  1.64 us (3%)
    pallas_call x10, Pallas kernels, visit(): pl.pallas_call(functools.partial(visit_kernel, half_inv, pairs, len(vis),...  21.3 us
    ppermute x2, starting transfers between devices, swapped(): lax.ppermute(value, 'blk', [(b, b + 1 - 2 * (b % 2)) for b in range(count)])  16.2 us
    ppermute x8, starting transfers between devices, toward(): return lax.ppermute(value, 'blk', pairs)  6.98 us
    ppermute x8, waiting for transfers between devices, toward(): return lax.ppermute(value, 'blk', pairs)  2.22 us
  transfers between devices with their start and end apart: 10, of which 6 were waited for; matrix products, arithmetic and copies ran while one was open for 0% of the time, Pallas kernels for 40%

profile of v4, /device:TPU:69, one launch (start us, length us, event | category | flops | bytes accessed | tf_op | source)
XLA Modules:
  0.0 49.7 jit_solution(13743591668000249647)
XLA Ops:
  0.0 0.9 %broadcast_multiply_fusion.coords = f32[32,768]{1,0:T(8,128)S(1)} fusion(f32[32,768]{1,0:T(8,128)} %param.5), kind=kLoop, calls=%fused_computation.1 | loop fusion | flops 24576 | bytes 196608 | tf_op jit(solution)/shard_map/mul | solution.py:224
  1.0 10.0 %collective-permute-start.1 = (f32[64,768]{1,0:T(8,128)S(1)}, f32[64,768]{1,0:T(8,128)S(1)}, u32[]{:S(2)}, u32[]{:S(2)}) collective-permute-start(f32[64,768]{1,0:T(8,128)S(1)} %field.1.refs_5_), channel_id=1, source_target_pairs={{0,1},{1,0},{2,3},{3,2},{4,5},{5,4},{6,7},{7,6},{8,9},{9,8},{10,11... | collective-permute-start | bytes 589832 | tf_op jit(solution)/shard_map/ppermute | solution.py:267
  11.2 0.9 %collective-permute-done.1.refs_1_.refs_5_ = f32[64,768]{1,0:T(8,128)S(1)} collective-permute-done((f32[64,768]{1,0:T(8,128)S(1)}, f32[64,768]{1,0:T(8,128)S(1)}, u32[]{:S(2)}, u32[]{:S(2)}) %collective-permute-start.1) | collective-permute-done | bytes 196640 | tf_op jit(solution)/shard_map/ppermute | solution.py:267
  12.1 1.5 %visit.10 = (f32[80,768]{1,0:T(8,128)S(1)}, bf16[144,768]{1,0:T(8,128)(2,1)S(1)}, bf16[128,768]{1,0:T(8,128)(2,1)S(1)}) custom-call(f32[64,128]{1,0:T(8,128)S(1)} %get-tuple-element.43.refs_0_, f32[64,768]{1,0:T(8,128)S(1)} %collective-permute-done.1.refs_1_.refs_5_, bf16[144,768]{1,0:T(8,128)(2,1)S(1)} %get-tuple-element.47.refs_2_, ...), custom_call_target="tpu_custom_call" | custom-call | flops 1000000000 | bytes 1000000 | tf_op jit(solution)/shard_map/visit/pallas_call | solution.py:194
  13.6 4.2 %collective-permute-start.5 = (f32[64,768]{1,0:T(8,128)S(1)}, f32[64,768]{1,0:T(8,128)S(1)}, u32[]{:S(2)}, u32[]{:S(2)}) collective-permute-start(f32[64,768]{1,0:T(8,128)S(1)} %field.1.refs_5_), channel_id=1, source_target_pairs={{0,3},{1,30},{2,5},{3,0},{4,7},{5,2},{6,9},{7,4},{8,11},{9,6},{10,... | collective-permute-start | bytes 589832 | tf_op jit(solution)/shard_map/ppermute | solution.py:273
  17.8 0.5 collective-permute-start.2
  18.3 2.5 %visit.11 = (f32[80,768]{1,0:T(8,128)S(1)}, f32[80,768]{1,0:T(8,128)S(1)}) custom-call(f32[64,128]{1,0:T(8,128)S(1)} %get-tuple-element.43.refs_0_, f32[64,768]{1,0:T(8,128)S(1)} %collective-permute-done.refs_1_, bf16[144,768]{1,0:T(8,128)(2,1)S(1)} %get-tuple-element.47.refs_2_, ...), custom_call_target="tpu_custom_call", output_to_operand_aliasing={{0}: (6, {})} | custom-call | flops 2000000000 | bytes 1000000 | tf_op jit(solution)/shard_map/visit/pallas_call | solution.py:194
  20.8 0.2 collective-permute-done.5.refs_1_
  21.1 1.5 %collective-permute-start.6 = (f32[64,768]{1,0:T(8,128)S(1)}, f32[64,768]{1,0:T(8,128)S(1)}, u32[]{:S(2)}, u32[]{:S(2)}) collective-permute-start(f32[64,768]{1,0:T(8,128)S(1)} %collective-permute-done.5.refs_1_), channel_id=1, source_target_pairs={{0,30},{1,3},{2,0},{3,5},{4,2},{5,7},{6,4},{7,9},{8,6},{9,11},{10,... | collective-permute-start | bytes 589832 | tf_op jit(solution)/shard_map/ppermute | solution.py:273
  22.6 2.6 %visit.12 = (f32[80,768]{1,0:T(8,128)S(1)}, f32[80,768]{1,0:T(8,128)S(1)}) custom-call(f32[64,128]{1,0:T(8,128)S(1)} %get-tuple-element.43.refs_0_, f32[64,768]{1,0:T(8,128)S(1)} %collective-permute-done.5.refs_1_, bf16[144,768]{1,0:T(8,128)(2,1)S(1)} %get-tuple-element.47.refs_2_, ...), custom_call_target="tpu_custom_call", output_to_operand_aliasing={{0}: (6, {}), {1}: (7, {})} | custom-call | flops 2000000000 | bytes 1000000 | tf_op jit(solution)/shard_map/visit/pallas_call | solution.py:194
  25.3 2.6 %visit.13 = (f32[80,768]{1,0:T(8,128)S(1)}, f32[80,768]{1,0:T(8,128)S(1)}) custom-call(f32[64,128]{1,0:T(8,128)S(1)} %get-tuple-element.43.refs_0_, f32[64,768]{1,0:T(8,128)S(1)} %collective-permute-done.2.refs_1_, bf16[144,768]{1,0:T(8,128)(2,1)S(1)} %get-tuple-element.47.refs_2_, ...), custom_call_target="tpu_custom_call", output_to_operand_aliasing={{0}: (6, {}), {1}: (7, {})} | custom-call | flops 2000000000 | bytes 1000000 | tf_op jit(solution)/shard_map/visit/pallas_call | solution.py:194
  27.9 0.3 collective-permute-start.7
  28.2 2.6 %visit.14 = (f32[80,768]{1,0:T(8,128)S(1)}, f32[80,768]{1,0:T(8,128)S(1)}) custom-call(f32[64,128]{1,0:T(8,128)S(1)} %get-tuple-element.43.refs_0_, f32[64,768]{1,0:T(8,128)S(1)} %collective-permute-done.6.refs_1_, bf16[144,768]{1,0:T(8,128)(2,1)S(1)} %get-tuple-element.47.refs_2_, ...), custom_call_target="tpu_custom_call", output_to_operand_aliasing={{0}: (6, {}), {1}: (7, {})} | custom-call | flops 2000000000 | bytes 1000000 | tf_op jit(solution)/shard_map/visit/pallas_call | solution.py:194
  30.8 0.2 collective-permute-done.3.refs_1_
  31.1 2.6 %visit.15 = (f32[80,768]{1,0:T(8,128)S(1)}, f32[80,768]{1,0:T(8,128)S(1)}) custom-call(f32[64,128]{1,0:T(8,128)S(1)} %get-tuple-element.43.refs_0_, f32[64,768]{1,0:T(8,128)S(1)} %collective-permute-done.3.refs_1_, bf16[144,768]{1,0:T(8,128)(2,1)S(1)} %get-tuple-element.47.refs_2_, ...), custom_call_target="tpu_custom_call", output_to_operand_aliasing={{0}: (6, {}), {1}: (7, {})} | custom-call | flops 2000000000 | bytes 1000000 | tf_op jit(solution)/shard_map/visit/pallas_call | solution.py:194
  33.6 0.3 collective-permute-done.7.refs_1_
  33.9 0.4 collective-permute-start.8
  34.3 2.6 %visit.16 = (f32[80,768]{1,0:T(8,128)S(1)}, f32[80,768]{1,0:T(8,128)S(1)}) custom-call(f32[64,128]{1,0:T(8,128)S(1)} %get-tuple-element.43.refs_0_, f32[64,768]{1,0:T(8,128)S(1)} %collective-permute-done.7.refs_1_, bf16[144,768]{1,0:T(8,128)(2,1)S(1)} %get-tuple-element.47.refs_2_, ...), custom_call_target="tpu_custom_call", output_to_operand_aliasing={{0}: (6, {}), {1}: (7, {})} | custom-call | flops 2000000000 | bytes 1000000 | tf_op jit(solution)/shard_map/visit/pallas_call | solution.py:194
  36.9 1.5 %visit.18.refs_4_ = f32[80,768]{1,0:T(8,128)S(1)} custom-call(f32[64,128]{1,0:T(8,128)S(1)} %get-tuple-element.43.refs_0_, f32[64,768]{1,0:T(8,128)S(1)} %collective-permute-done.4.refs_1_, bf16[144,768]{1,0:T(8,128)(2,1)S(1)} %get-tuple-element.53.refs_4_.refs_2_, ...), custom_call_target="tpu_custom_call", output_to_operand_aliasing={{}: (4, {})} | custom-call | flops 1000000000 | bytes 1000000 | tf_op jit(solution)/shard_map/visit/pallas_call | solution.py:194
  38.4 1.3 %collective-permute-done.8.refs_1_ = f32[64,768]{1,0:T(8,128)S(1)} collective-permute-done((f32[64,768]{1,0:T(8,128)S(1)}, f32[64,768]{1,0:T(8,128)S(1)}, u32[]{:S(2)}, u32[]{:S(2)}) %collective-permute-start.8) | collective-permute-done | bytes 196640 | tf_op jit(solution)/shard_map/ppermute | solution.py:273
  39.7 1.5 %visit.19 = (f32[80,768]{1,0:T(8,128)S(1)}, f32[32,768]{1,0:T(8,128)S(1)}) custom-call(f32[64,128]{1,0:T(8,128)S(1)} %get-tuple-element.43.refs_0_, f32[64,768]{1,0:T(8,128)S(1)} %collective-permute-done.8.refs_1_, bf16[144,768]{1,0:T(8,128)(2,1)S(1)} %get-tuple-element.53.refs_4_.refs_2_, ...), custom_call_target="tpu_custom_call", output_to_operand_aliasing={{0}: (4, {})} | custom-call | flops 1000000000 | bytes 1000000 | tf_op jit(solution)/shard_map/visit/pallas_call | solution.py:194
  41.2 6.2 %collective-permute-start.9 = (f32[32,768]{1,0:T(8,128)S(1)}, f32[32,768]{1,0:T(8,128)S(1)}, u32[]{:S(2)}, u32[]{:S(2)}) collective-permute-start(f32[32,768]{1,0:T(8,128)S(1)} %get-tuple-element.80), channel_id=1, source_target_pairs={{0,1},{1,0},{2,3},{3,2},{4,5},{5,4},{6,7},{7,6},{8,9},{9,8},{10,11... | collective-permute-start | bytes 294920 | tf_op jit(solution)/shard_map/ppermute | solution.py:267
  47.4 1.5 %visit.17 = (f32[80,768]{1,0:T(8,128)S(1)}, f32[32,768]{1,0:T(8,128)S(1)}) custom-call(f32[64,128]{1,0:T(8,128)S(1)} %get-tuple-element.43.refs_0_, f32[64,768]{1,0:T(8,128)S(1)} %collective-permute-done.4.refs_1_, bf16[144,768]{1,0:T(8,128)(2,1)S(1)} %get-tuple-element.47.refs_2_, ...), custom_call_target="tpu_custom_call", output_to_operand_aliasing={{0}: (4, {})} | custom-call | flops 1000000000 | bytes 1000000 | tf_op jit(solution)/shard_map/visit/pallas_call | solution.py:194
  49.0 0.7 %add_multiply_fusion = f32[32,768]{1,0:T(8,128)} fusion(f32[32,768]{1,0:T(8,128)S(1)} %get-tuple-element.76, f32[32,768]{1,0:T(8,128)S(1)} %collective-permute-done.9, f32[32]{0:T(128)S(1)} %broadcast_divide_fusion), kind=kLoop, calls=%fused_computation | loop fusion | flops 49152 | bytes 295040 | tf_op jit(solution)/shard_map/mul | solution.py:302
  (19 shorter events, 0.5 us)
Async XLA Ops:
  0.0 0.9 %copy-start = (f32[15,768]{1,0:T(8,128)S(1)}, f32[15,768]{1,0:T(8,128)}, u32[]{:S(2)}) copy-start(f32[15,768]{1,0:T(8,128)} %solves.1) | copy-start | bytes 138244
  0.0 0.9 %copy-start.1 = (f32[15,768]{1,0:T(8,128)S(1)}, f32[15,768]{1,0:T(8,128)}, u32[]{:S(2)}) copy-start(f32[15,768]{1,0:T(8,128)} %probes.1) | copy-start | bytes 138244
  0.0 0.9 %copy-start.2 = (f32[768]{0:T(1024)S(1)}, f32[768]{0:T(1024)}, u32[]{:S(2)}) copy-start(f32[768]{0:T(1024)} %param.6) | copy-start | bytes 9220
  1.0 10.0 %copy-start.3 = (f32[32]{0:T(128)S(1)}, f32[32]{0:T(128)}, u32[]{:S(2)}) copy-start(f32[32]{0:T(128)} %param.9) | copy-start | bytes 388
  1.0 11.1 %collective-permute-start.1 = (f32[64,768]{1,0:T(8,128)S(1)}, f32[64,768]{1,0:T(8,128)S(1)}, u32[]{:S(2)}, u32[]{:S(2)}) collective-permute-start(f32[64,768]{1,0:T(8,128)S(1)} %field.1.refs_5_), channel_id=1, source_target_pairs={{0,1},{1,0},{2,3},{3,2},{4,5},{5,4},{6,7},{7,6},{8,9},{9,8},{10,11... | collective-permute-start | bytes 589832 | tf_op jit(solution)/shard_map/ppermute | solution.py:267
  11.0 6.8 %collective-permute-start = (f32[64,768]{1,0:T(8,128)S(1)}, f32[64,768]{1,0:T(8,128)S(1)}, u32[]{:S(2)}, u32[]{:S(2)}) collective-permute-start(f32[64,768]{1,0:T(8,128)S(1)} %field.1.refs_5_), channel_id=1, source_target_pairs={{0,30},{1,3},{2,0},{3,5},{4,2},{5,7},{6,4},{7,9},{8,6},{9,11},{10,... | collective-permute-start | bytes 589832 | tf_op jit(solution)/shard_map/ppermute | solution.py:273
  13.6 7.5 %collective-permute-start.5 = (f32[64,768]{1,0:T(8,128)S(1)}, f32[64,768]{1,0:T(8,128)S(1)}, u32[]{:S(2)}, u32[]{:S(2)}) collective-permute-start(f32[64,768]{1,0:T(8,128)S(1)} %field.1.refs_5_), channel_id=1, source_target_pairs={{0,3},{1,30},{2,5},{3,0},{4,7},{5,2},{6,9},{7,4},{8,11},{9,6},{10,... | collective-permute-start | bytes 589832 | tf_op jit(solution)/shard_map/ppermute | solution.py:273
  17.8 7.4 %collective-permute-start.2 = (f32[64,768]{1,0:T(8,128)S(1)}, f32[64,768]{1,0:T(8,128)S(1)}, u32[]{:S(2)}, u32[]{:S(2)}) collective-permute-start(f32[64,768]{1,0:T(8,128)S(1)} %collective-permute-done.refs_1_), channel_id=1, source_target_pairs={{0,30},{1,3},{2,0},{3,5},{4,2},{5,7},{6,4},{7,9},{8,6},{9,11},{10,... | collective-permute-start | bytes 589832 | tf_op jit(solution)/shard_map/ppermute | solution.py:273
  21.1 6.8 %collective-permute-start.6 = (f32[64,768]{1,0:T(8,128)S(1)}, f32[64,768]{1,0:T(8,128)S(1)}, u32[]{:S(2)}, u32[]{:S(2)}) collective-permute-start(f32[64,768]{1,0:T(8,128)S(1)} %collective-permute-done.5.refs_1_), channel_id=1, source_target_pairs={{0,30},{1,3},{2,0},{3,5},{4,2},{5,7},{6,4},{7,9},{8,6},{9,11},{10,... | collective-permute-start | bytes 589832 | tf_op jit(solution)/shard_map/ppermute | solution.py:273
  25.2 5.8 %collective-permute-start.3 = (f32[64,768]{1,0:T(8,128)S(1)}, f32[64,768]{1,0:T(8,128)S(1)}, u32[]{:S(2)}, u32[]{:S(2)}) collective-permute-start(f32[64,768]{1,0:T(8,128)S(1)} %collective-permute-done.2.refs_1_), channel_id=1, source_target_pairs={{0,30},{1,3},{2,0},{3,5},{4,2},{5,7},{6,4},{7,9},{8,6},{9,11},{10,... | collective-permute-start | bytes 589832 | tf_op jit(solution)/shard_map/ppermute | solution.py:273
  27.9 6.0 %collective-permute-start.7 = (f32[64,768]{1,0:T(8,128)S(1)}, f32[64,768]{1,0:T(8,128)S(1)}, u32[]{:S(2)}, u32[]{:S(2)}) collective-permute-start(f32[64,768]{1,0:T(8,128)S(1)} %collective-permute-done.6.refs_1_), channel_id=1, source_target_pairs={{0,30},{1,3},{2,0},{3,5},{4,2},{5,7},{6,4},{7,9},{8,6},{9,11},{10,... | collective-permute-start | bytes 589832 | tf_op jit(solution)/shard_map/ppermute | solution.py:273
  31.0 5.9 %collective-permute-start.4 = (f32[64,768]{1,0:T(8,128)S(1)}, f32[64,768]{1,0:T(8,128)S(1)}, u32[]{:S(2)}, u32[]{:S(2)}) collective-permute-start(f32[64,768]{1,0:T(8,128)S(1)} %collective-permute-done.3.refs_1_), channel_id=1, source_target_pairs={{0,30},{1,3},{2,0},{3,5},{4,2},{5,7},{6,4},{7,9},{8,6},{9,11},{10,... | collective-permute-start | bytes 589832 | tf_op jit(solution)/shard_map/ppermute | solution.py:273
  33.9 5.7 %collective-permute-start.8 = (f32[64,768]{1,0:T(8,128)S(1)}, f32[64,768]{1,0:T(8,128)S(1)}, u32[]{:S(2)}, u32[]{:S(2)}) collective-permute-start(f32[64,768]{1,0:T(8,128)S(1)} %collective-permute-done.7.refs_1_), channel_id=1, source_target_pairs={{0,30},{1,3},{2,0},{3,5},{4,2},{5,7},{6,4},{7,9},{8,6},{9,11},{10,... | collective-permute-start | bytes 589832 | tf_op jit(solution)/shard_map/ppermute | solution.py:273
  41.2 7.8 %collective-permute-start.9 = (f32[32,768]{1,0:T(8,128)S(1)}, f32[32,768]{1,0:T(8,128)S(1)}, u32[]{:S(2)}, u32[]{:S(2)}) collective-permute-start(f32[32,768]{1,0:T(8,128)S(1)} %get-tuple-element.80), channel_id=1, source_target_pairs={{0,1},{1,0},{2,3},{3,2},{4,5},{5,4},{6,7},{7,6},{8,9},{9,8},{10,11... | collective-permute-start | bytes 294920 | tf_op jit(solution)/shard_map/ppermute | solution.py:267

commit v5 on v4

--- a/solution.py
+++ b/solution.py
@@ -202,7 +202,7 @@
         input_output_aliases={first + index: index for index in range(len(accs))},
         compiler_params=pltpu.CompilerParams(vmem_limit_bytes=20 * 2**20),
         cost_estimate=pl.CostEstimate(
-            flops=len(pairs) * 10**9, bytes_accessed=10**6, transcendentals=0
+            flops=2 * 10**9, bytes_accessed=10**6, transcendentals=0
         ),
         name="visit",
     )(*args)
@@ -289,13 +289,16 @@
     for hop in range(1, hops):
         here, there = near, cross
         near = toward(here, -2, 2)
-        accs = visit(half_inv, scale, ((0, 1), (0, 0)), [here], [own, own_mate], accs)
+        if hop < hops - 1:
+            accs = visit(half_inv, scale, ((0, 1), (0, 0)), [here], [own, own_mate], accs)
+        else:
+            accs = accs[:1] + visit(half_inv, scale, ((0, 0),), [here], [own_mate], accs[1:])
         there, near_accs = lax.optimization_barrier((there, accs))
         cross = toward(there, -2, 2)
         accs = visit(half_inv, scale, ((0, 1), (0, 0)), [there], [own, own_mate], near_accs)
-    (acc,) = visit(half_inv, scale, ((0, 0),), [near], [own_mate], accs[1:])
-    cross, acc = lax.optimization_barrier((cross, acc))
-    _, theirs = visit(half_inv, scale, ((0, 0),), [cross], [own_mate], [acc], done=(0,), fields=[mate])
+    accs = visit(half_inv, scale, ((0, 1), (1, 0)), [near, here], [own, own_mate], accs)
+    cross, *accs = lax.optimization_barrier((cross, *accs))
+    _, theirs = visit(half_inv, scale, ((0, 0),), [cross], [own_mate], accs[1:], done=(0,), fields=[mate])
     theirs = swapped(theirs)
     _, mine = visit(half_inv, scale, ((0, 0),), [near], [own], accs[:1], done=(0,), fields=[field])
     total = mine + theirs

time: 49.8 us -> 48.6 us (0.976)
  starting transfers between devices: 23.2 us -> 21.7 us
    ppermute x2, starting transfers between devices: 16.2 us -> 15.1 us  [swapped(): lax.ppermute(value, 'blk', [(b, b + 1 - 2 * (b % 2)) for b in range(count)])]
  transfers between devices with their start and end apart: 10 -> 10, of which waited for: 6 -> 7; matrix products, arithmetic and copies ran while one was open for 0% -> 0% of each run, Pallas kernels for 40% -> 41%
where the time goes in v5:
time: 48.6 us; the launch traced here: 48.5 us
  starting transfers between devices  21.7 us (45%)
  Pallas kernels  21.6 us (44%)
  waiting for transfers between devices  3.41 us (7%)
  other arithmetic  1.64 us (3%)
    pallas_call x10, Pallas kernels, visit(): pl.pallas_call(functools.partial(visit_kernel, half_inv, pairs, len(vis),...  21.4 us
    ppermute x2, starting transfers between devices, swapped(): lax.ppermute(value, 'blk', [(b, b + 1 - 2 * (b % 2)) for b in range(count)])  15.1 us
    ppermute x8, starting transfers between devices, toward(): return lax.ppermute(value, 'blk', pairs)  6.59 us
    ppermute x8, waiting for transfers between devices, toward(): return lax.ppermute(value, 'blk', pairs)  2.49 us
  transfers between devices with their start and end apart: 10, of which 7 were waited for; matrix products, arithmetic and copies ran while one was open for 0% of the time, Pallas kernels for 41%

profile of v5, /device:TPU:69, one launch (start us, length us, event | category | flops | bytes accessed | tf_op | source)
XLA Modules:
  0.0 48.5 jit_solution(15420906722751863200)
XLA Ops:
  0.0 0.9 %broadcast_multiply_fusion.coords = f32[32,768]{1,0:T(8,128)S(1)} fusion(f32[32,768]{1,0:T(8,128)} %param.5), kind=kLoop, calls=%fused_computation.1 | loop fusion | flops 24576 | bytes 196608 | tf_op jit(solution)/shard_map/mul | solution.py:224
  1.0 10.0 %collective-permute-start.1 = (f32[64,768]{1,0:T(8,128)S(1)}, f32[64,768]{1,0:T(8,128)S(1)}, u32[]{:S(2)}, u32[]{:S(2)}) collective-permute-start(f32[64,768]{1,0:T(8,128)S(1)} %field.1.refs_5_), channel_id=1, source_target_pairs={{0,1},{1,0},{2,3},{3,2},{4,5},{5,4},{6,7},{7,6},{8,9},{9,8},{10,11... | collective-permute-start | bytes 589832 | tf_op jit(solution)/shard_map/ppermute | solution.py:267
  11.2 0.9 %collective-permute-done.1.refs_1_.refs_5_ = f32[64,768]{1,0:T(8,128)S(1)} collective-permute-done((f32[64,768]{1,0:T(8,128)S(1)}, f32[64,768]{1,0:T(8,128)S(1)}, u32[]{:S(2)}, u32[]{:S(2)}) %collective-permute-start.1) | collective-permute-done | bytes 196640 | tf_op jit(solution)/shard_map/ppermute | solution.py:267
  12.1 1.5 %visit.10 = (f32[80,768]{1,0:T(8,128)S(1)}, bf16[144,768]{1,0:T(8,128)(2,1)S(1)}, bf16[128,768]{1,0:T(8,128)(2,1)S(1)}) custom-call(f32[64,128]{1,0:T(8,128)S(1)} %get-tuple-element.44.refs_0_, f32[64,768]{1,0:T(8,128)S(1)} %collective-permute-done.1.refs_1_.refs_5_, bf16[144,768]{1,0:T(8,128)(2,1)S(1)} %get-tuple-element.48.refs_2_.refs_3_, ...), custom_call_target="tpu_custom_call" | custom-call | flops 2000000000 | bytes 1000000 | tf_op jit(solution)/shard_map/visit/pallas_call | solution.py:194
  13.5 4.2 %collective-permute-start.5 = (f32[64,768]{1,0:T(8,128)S(1)}, f32[64,768]{1,0:T(8,128)S(1)}, u32[]{:S(2)}, u32[]{:S(2)}) collective-permute-start(f32[64,768]{1,0:T(8,128)S(1)} %field.1.refs_5_), channel_id=1, source_target_pairs={{0,3},{1,30},{2,5},{3,0},{4,7},{5,2},{6,9},{7,4},{8,11},{9,6},{10,... | collective-permute-start | bytes 589832 | tf_op jit(solution)/shard_map/ppermute | solution.py:273
  17.8 0.5 collective-permute-start.2
  18.3 2.5 %visit.11 = (f32[80,768]{1,0:T(8,128)S(1)}, f32[80,768]{1,0:T(8,128)S(1)}) custom-call(f32[64,128]{1,0:T(8,128)S(1)} %get-tuple-element.44.refs_0_, f32[64,768]{1,0:T(8,128)S(1)} %collective-permute-done.refs_1_, bf16[144,768]{1,0:T(8,128)(2,1)S(1)} %get-tuple-element.48.refs_2_.refs_3_, ...), custom_call_target="tpu_custom_call", output_to_operand_aliasing={{0}: (6, {})} | custom-call | flops 2000000000 | bytes 1000000 | tf_op jit(solution)/shard_map/visit/pallas_call | solution.py:194
  20.8 0.2 collective-permute-done.5.refs_1_
  21.1 1.5 %collective-permute-start.6 = (f32[64,768]{1,0:T(8,128)S(1)}, f32[64,768]{1,0:T(8,128)S(1)}, u32[]{:S(2)}, u32[]{:S(2)}) collective-permute-start(f32[64,768]{1,0:T(8,128)S(1)} %collective-permute-done.5.refs_1_), channel_id=1, source_target_pairs={{0,30},{1,3},{2,0},{3,5},{4,2},{5,7},{6,4},{7,9},{8,6},{9,11},{10,... | collective-permute-start | bytes 589832 | tf_op jit(solution)/shard_map/ppermute | solution.py:273
  22.6 2.6 %visit.12 = (f32[80,768]{1,0:T(8,128)S(1)}, f32[80,768]{1,0:T(8,128)S(1)}) custom-call(f32[64,128]{1,0:T(8,128)S(1)} %get-tuple-element.44.refs_0_, f32[64,768]{1,0:T(8,128)S(1)} %collective-permute-done.5.refs_1_, bf16[144,768]{1,0:T(8,128)(2,1)S(1)} %get-tuple-element.48.refs_2_.refs_3_, ...), custom_call_target="tpu_custom_call", output_to_operand_aliasing={{0}: (6, {}), {1}: (7, {})} | custom-call | flops 2000000000 | bytes 1000000 | tf_op jit(solution)/shard_map/visit/pallas_call | solution.py:194
  25.3 2.6 %visit.13 = (f32[80,768]{1,0:T(8,128)S(1)}, f32[80,768]{1,0:T(8,128)S(1)}) custom-call(f32[64,128]{1,0:T(8,128)S(1)} %get-tuple-element.44.refs_0_, f32[64,768]{1,0:T(8,128)S(1)} %collective-permute-done.2.refs_1_, bf16[144,768]{1,0:T(8,128)(2,1)S(1)} %get-tuple-element.48.refs_2_.refs_3_, ...), custom_call_target="tpu_custom_call", output_to_operand_aliasing={{0}: (6, {}), {1}: (7, {})} | custom-call | flops 2000000000 | bytes 1000000 | tf_op jit(solution)/shard_map/visit/pallas_call | solution.py:194
  27.9 0.3 collective-permute-start.7
  28.2 2.6 %visit.14 = (f32[80,768]{1,0:T(8,128)S(1)}, f32[80,768]{1,0:T(8,128)S(1)}) custom-call(f32[64,128]{1,0:T(8,128)S(1)} %get-tuple-element.44.refs_0_, f32[64,768]{1,0:T(8,128)S(1)} %collective-permute-done.6.refs_1_, bf16[144,768]{1,0:T(8,128)(2,1)S(1)} %get-tuple-element.48.refs_2_.refs_3_, ...), custom_call_target="tpu_custom_call", output_to_operand_aliasing={{0}: (6, {}), {1}: (7, {})} | custom-call | flops 2000000000 | bytes 1000000 | tf_op jit(solution)/shard_map/visit/pallas_call | solution.py:194
  30.8 0.2 collective-permute-done.3.refs_1_.refs_2_
  31.0 1.5 %visit.15.refs_7_ = f32[80,768]{1,0:T(8,128)S(1)} custom-call(f32[64,128]{1,0:T(8,128)S(1)} %get-tuple-element.44.refs_0_, f32[64,768]{1,0:T(8,128)S(1)} %collective-permute-done.3.refs_1_.refs_2_, bf16[144,768]{1,0:T(8,128)(2,1)S(1)} %get-tuple-element.54.refs_4_.refs_2_.refs_5_, ...), custom_call_target="tpu_custom_call", output_to_operand_aliasing={{}: (4, {})} | custom-call | flops 2000000000 | bytes 1000000 | tf_op jit(solution)/shard_map/visit/pallas_call | solution.py:194
  32.5 1.4 %collective-permute-done.7.refs_1_ = f32[64,768]{1,0:T(8,128)S(1)} collective-permute-done((f32[64,768]{1,0:T(8,128)S(1)}, f32[64,768]{1,0:T(8,128)S(1)}, u32[]{:S(2)}, u32[]{:S(2)}) %collective-permute-start.7) | collective-permute-done | bytes 196640 | tf_op jit(solution)/shard_map/ppermute | solution.py:273
  33.9 2.6 %visit.16 = (f32[80,768]{1,0:T(8,128)S(1)}, f32[80,768]{1,0:T(8,128)S(1)}) custom-call(f32[64,128]{1,0:T(8,128)S(1)} %get-tuple-element.44.refs_0_, f32[64,768]{1,0:T(8,128)S(1)} %collective-permute-done.7.refs_1_, bf16[144,768]{1,0:T(8,128)(2,1)S(1)} %get-tuple-element.48.refs_2_.refs_3_, ...), custom_call_target="tpu_custom_call", output_to_operand_aliasing={{0}: (6, {}), {1}: (7, {})} | custom-call | flops 2000000000 | bytes 1000000 | tf_op jit(solution)/shard_map/visit/pallas_call | solution.py:194
  36.5 0.3 collective-permute-done.4.refs_1_
  36.8 2.7 %visit.17 = (f32[80,768]{1,0:T(8,128)S(1)}, f32[80,768]{1,0:T(8,128)S(1)}) custom-call(f32[64,128]{1,0:T(8,128)S(1)} %get-tuple-element.44.refs_0_, f32[64,768]{1,0:T(8,128)S(1)} %collective-permute-done.4.refs_1_, f32[64,768]{1,0:T(8,128)S(1)} %collective-permute-done.3.refs_1_.refs_2_, ...), custom_call_target="tpu_custom_call", output_to_operand_aliasing={{0}: (7, {}), {1}: (8, {})} | custom-call | flops 2000000000 | bytes 1000000 | tf_op jit(solution)/shard_map/visit/pallas_call | solution.py:194
  39.5 0.2 collective-permute-done.8.refs_1_
  39.6 1.5 %visit.19 = (f32[80,768]{1,0:T(8,128)S(1)}, f32[32,768]{1,0:T(8,128)S(1)}) custom-call(f32[64,128]{1,0:T(8,128)S(1)} %get-tuple-element.44.refs_0_, f32[64,768]{1,0:T(8,128)S(1)} %collective-permute-done.8.refs_1_, bf16[144,768]{1,0:T(8,128)(2,1)S(1)} %get-tuple-element.54.refs_4_.refs_2_.refs_5_, ...), custom_call_target="tpu_custom_call", output_to_operand_aliasing={{0}: (4, {})} | custom-call | flops 2000000000 | bytes 1000000 | tf_op jit(solution)/shard_map/visit/pallas_call | solution.py:194
  41.2 5.1 %collective-permute-start.9 = (f32[32,768]{1,0:T(8,128)S(1)}, f32[32,768]{1,0:T(8,128)S(1)}, u32[]{:S(2)}, u32[]{:S(2)}) collective-permute-start(f32[32,768]{1,0:T(8,128)S(1)} %get-tuple-element.82), channel_id=1, source_target_pairs={{0,1},{1,0},{2,3},{3,2},{4,5},{5,4},{6,7},{7,6},{8,9},{9,8},{10,11... | collective-permute-start | bytes 294920 | tf_op jit(solution)/shard_map/ppermute | solution.py:267
  46.3 1.5 %visit.18 = (f32[80,768]{1,0:T(8,128)S(1)}, f32[32,768]{1,0:T(8,128)S(1)}) custom-call(f32[64,128]{1,0:T(8,128)S(1)} %get-tuple-element.44.refs_0_, f32[64,768]{1,0:T(8,128)S(1)} %collective-permute-done.4.refs_1_, bf16[144,768]{1,0:T(8,128)(2,1)S(1)} %get-tuple-element.48.refs_2_.refs_3_, ...), custom_call_target="tpu_custom_call", output_to_operand_aliasing={{0}: (4, {})} | custom-call | flops 2000000000 | bytes 1000000 | tf_op jit(solution)/shard_map/visit/pallas_call | solution.py:194
  47.8 0.7 %add_multiply_fusion = f32[32,768]{1,0:T(8,128)} fusion(f32[32,768]{1,0:T(8,128)S(1)} %get-tuple-element.79, f32[32,768]{1,0:T(8,128)S(1)} %collective-permute-done.9, f32[32]{0:T(128)S(1)} %broadcast_divide_fusion), kind=kLoop, calls=%fused_computation | loop fusion | flops 49152 | bytes 295040 | tf_op jit(solution)/shard_map/mul | solution.py:305
  (19 shorter events, 0.5 us)
Async XLA Ops:
  0.0 0.9 %copy-start = (f32[15,768]{1,0:T(8,128)S(1)}, f32[15,768]{1,0:T(8,128)}, u32[]{:S(2)}) copy-start(f32[15,768]{1,0:T(8,128)} %solves.1) | copy-start | bytes 138244
  0.0 0.9 %copy-start.1 = (f32[15,768]{1,0:T(8,128)S(1)}, f32[15,768]{1,0:T(8,128)}, u32[]{:S(2)}) copy-start(f32[15,768]{1,0:T(8,128)} %probes.1) | copy-start | bytes 138244
  0.0 0.9 %copy-start.2 = (f32[768]{0:T(1024)S(1)}, f32[768]{0:T(1024)}, u32[]{:S(2)}) copy-start(f32[768]{0:T(1024)} %param.6) | copy-start | bytes 9220
  1.0 10.0 %copy-start.3 = (f32[32]{0:T(128)S(1)}, f32[32]{0:T(128)}, u32[]{:S(2)}) copy-start(f32[32]{0:T(128)} %param.9) | copy-start | bytes 388
  1.0 11.1 %collective-permute-start.1 = (f32[64,768]{1,0:T(8,128)S(1)}, f32[64,768]{1,0:T(8,128)S(1)}, u32[]{:S(2)}, u32[]{:S(2)}) collective-permute-start(f32[64,768]{1,0:T(8,128)S(1)} %field.1.refs_5_), channel_id=1, source_target_pairs={{0,1},{1,0},{2,3},{3,2},{4,5},{5,4},{6,7},{7,6},{8,9},{9,8},{10,11... | collective-permute-start | bytes 589832 | tf_op jit(solution)/shard_map/ppermute | solution.py:267
  11.0 6.8 %collective-permute-start = (f32[64,768]{1,0:T(8,128)S(1)}, f32[64,768]{1,0:T(8,128)S(1)}, u32[]{:S(2)}, u32[]{:S(2)}) collective-permute-start(f32[64,768]{1,0:T(8,128)S(1)} %field.1.refs_5_), channel_id=1, source_target_pairs={{0,30},{1,3},{2,0},{3,5},{4,2},{5,7},{6,4},{7,9},{8,6},{9,11},{10,... | collective-permute-start | bytes 589832 | tf_op jit(solution)/shard_map/ppermute | solution.py:273
  13.5 7.5 %collective-permute-start.5 = (f32[64,768]{1,0:T(8,128)S(1)}, f32[64,768]{1,0:T(8,128)S(1)}, u32[]{:S(2)}, u32[]{:S(2)}) collective-permute-start(f32[64,768]{1,0:T(8,128)S(1)} %field.1.refs_5_), channel_id=1, source_target_pairs={{0,3},{1,30},{2,5},{3,0},{4,7},{5,2},{6,9},{7,4},{8,11},{9,6},{10,... | collective-permute-start | bytes 589832 | tf_op jit(solution)/shard_map/ppermute | solution.py:273
  17.8 7.3 %collective-permute-start.2 = (f32[64,768]{1,0:T(8,128)S(1)}, f32[64,768]{1,0:T(8,128)S(1)}, u32[]{:S(2)}, u32[]{:S(2)}) collective-permute-start(f32[64,768]{1,0:T(8,128)S(1)} %collective-permute-done.refs_1_), channel_id=1, source_target_pairs={{0,30},{1,3},{2,0},{3,5},{4,2},{5,7},{6,4},{7,9},{8,6},{9,11},{10,... | collective-permute-start | bytes 589832 | tf_op jit(solution)/shard_map/ppermute | solution.py:273
  21.1 6.8 %collective-permute-start.6 = (f32[64,768]{1,0:T(8,128)S(1)}, f32[64,768]{1,0:T(8,128)S(1)}, u32[]{:S(2)}, u32[]{:S(2)}) collective-permute-start(f32[64,768]{1,0:T(8,128)S(1)} %collective-permute-done.5.refs_1_), channel_id=1, source_target_pairs={{0,30},{1,3},{2,0},{3,5},{4,2},{5,7},{6,4},{7,9},{8,6},{9,11},{10,... | collective-permute-start | bytes 589832 | tf_op jit(solution)/shard_map/ppermute | solution.py:273
  25.2 5.8 %collective-permute-start.3 = (f32[64,768]{1,0:T(8,128)S(1)}, f32[64,768]{1,0:T(8,128)S(1)}, u32[]{:S(2)}, u32[]{:S(2)}) collective-permute-start(f32[64,768]{1,0:T(8,128)S(1)} %collective-permute-done.2.refs_1_), channel_id=1, source_target_pairs={{0,30},{1,3},{2,0},{3,5},{4,2},{5,7},{6,4},{7,9},{8,6},{9,11},{10,... | collective-permute-start | bytes 589832 | tf_op jit(solution)/shard_map/ppermute | solution.py:273
  27.9 6.0 %collective-permute-start.7 = (f32[64,768]{1,0:T(8,128)S(1)}, f32[64,768]{1,0:T(8,128)S(1)}, u32[]{:S(2)}, u32[]{:S(2)}) collective-permute-start(f32[64,768]{1,0:T(8,128)S(1)} %collective-permute-done.6.refs_1_), channel_id=1, source_target_pairs={{0,30},{1,3},{2,0},{3,5},{4,2},{5,7},{6,4},{7,9},{8,6},{9,11},{10,... | collective-permute-start | bytes 589832 | tf_op jit(solution)/shard_map/ppermute | solution.py:273
  31.0 5.7 %collective-permute-start.4 = (f32[64,768]{1,0:T(8,128)S(1)}, f32[64,768]{1,0:T(8,128)S(1)}, u32[]{:S(2)}, u32[]{:S(2)}) collective-permute-start(f32[64,768]{1,0:T(8,128)S(1)} %collective-permute-done.3.refs_1_.refs_2_), channel_id=1, source_target_pairs={{0,30},{1,3},{2,0},{3,5},{4,2},{5,7},{6,4},{7,9},{8,6},{9,11},{10,... | collective-permute-start | bytes 589832 | tf_op jit(solution)/shard_map/ppermute | solution.py:273
  33.9 5.7 %collective-permute-start.8 = (f32[64,768]{1,0:T(8,128)S(1)}, f32[64,768]{1,0:T(8,128)S(1)}, u32[]{:S(2)}, u32[]{:S(2)}) collective-permute-start(f32[64,768]{1,0:T(8,128)S(1)} %collective-permute-done.7.refs_1_), channel_id=1, source_target_pairs={{0,30},{1,3},{2,0},{3,5},{4,2},{5,7},{6,4},{7,9},{8,6},{9,11},{10,... | collective-permute-start | bytes 589832 | tf_op jit(solution)/shard_map/ppermute | solution.py:273
  41.2 6.6 %collective-permute-start.9 = (f32[32,768]{1,0:T(8,128)S(1)}, f32[32,768]{1,0:T(8,128)S(1)}, u32[]{:S(2)}, u32[]{:S(2)}) collective-permute-start(f32[32,768]{1,0:T(8,128)S(1)} %get-tuple-element.82), channel_id=1, source_target_pairs={{0,1},{1,0},{2,3},{3,2},{4,5},{5,4},{6,7},{7,6},{8,9},{9,8},{10,11... | collective-permute-start | bytes 294920 | tf_op jit(solution)/shard_map/ppermute | solution.py:267
